TPU v7x, 128 devices: a whole 4x4x4 slice. The times are simulated.
128 devices in a mesh: hi: 64 (over y_lo, x, z, core), grp: 2 (over y_hi).
Axes of the slice: x: 4, y: 4 (y_hi: 2, y_lo: 2; y = y_hi * 2 + y_lo), z: 4, core: 2. Of those that a mesh axis runs over, the one named last changes fastest.
Arguments:
- rho: float32 [2, 8192, 8192], P(None, ('hi', 'grp')), may hold values from -6 to 9
- perm: int32 [2, 13], replicated, may hold values from 0 to 12, each once within a row
- superop: float32 [2, 2, 16, 16], replicated, may hold values from -0.3 to 1.1
Outputs:
- rho_out: float32 [2, 8192, 8192], P(None, ('hi', 'grp'))
- trace_mean: float32 [], replicated
All inputs are finite; a program needn't handle non-finite values.
Results may differ from a plain program's by a relative error of at most 0.0001.
Values sent between devices are 32-bit elements; how exact they have to be, the bound alone decides.
No kernel may reach another device: no remote copies, remote signals or barrier semaphores. Data moves between devices by JAX's collectives and lax.ppermute only.
A program may use at most 256 MiB of HBM per device.

v0:
```python
import jax
import jax.numpy as jnp
from jax import lax
from jax.sharding import Mesh
from jax.sharding import PartitionSpec as P

ROWS = 8192
PAIRS = 2
HI_GRP = ("hi_0", "hi_1", "hi_2", "hi_3", "grp")


def in_blocks(array, dim, count):
    lengths = array.shape
    parts = array.reshape(*lengths[:dim], count, lengths[dim] // count, *lengths[dim + 1 :])
    return jnp.moveaxis(parts, dim, 0)


def piece_ends(length, count):
    unit = 8 if length >= 8 * count else 1
    return [length // unit * k // count * unit for k in range(1, count)]


def in_order(parts, dim):
    lengths = list(parts.shape[1:])
    lengths[dim] *= parts.shape[0]
    return jnp.moveaxis(parts, 0, dim).reshape(lengths)


def cut_exchange(array, axis, pieces, split_dim, concat_dim):
    parts = in_blocks(array, split_dim, lax.axis_size(axis))
    cut = max(range(1, max(2, parts.ndim - 1)), key=lambda d: parts.shape[d])
    done = []
    for share in jnp.split(parts, piece_ends(parts.shape[cut], pieces), axis=cut):
        if share.size:
            done.append(lax.all_to_all(share, axis, split_axis=0, concat_axis=0, tiled=True))
    return in_order(jnp.concatenate(done, axis=cut), concat_dim)


def by_axis(array, axes):
    for axis in axes:
        array = lax.psum(array, axis)
    return array


def relabel_table(order, count):
    positions = jnp.arange(count, dtype=jnp.int32)
    result = jnp.zeros((count,), jnp.int32)
    for qubit in range(order.shape[0]):
        bit_value = jnp.bitwise_and(jnp.right_shift(positions, qubit), 1)
        result = result + bit_value * jnp.left_shift(jnp.int32(1), order[qubit])
    return result


def apply_channel(matrix, layer_super, pairs):
    real_part = layer_super[0]
    imag_part = layer_super[1]
    kernel = jnp.stack(
        [jnp.stack([real_part, -imag_part], axis=1), jnp.stack([imag_part, real_part], axis=1)],
        axis=0,
    )
    kernel = kernel.reshape(32, 32)
    row_count = matrix.shape[1]
    col_count = matrix.shape[2]
    span = 4**pairs
    row_blocks = row_count // span
    col_blocks = col_count // span
    tile = matrix.reshape(2, row_blocks, span, col_blocks, span)
    tile = jnp.transpose(tile, (0, 2, 4, 1, 3)).reshape(2, span, span, row_blocks * col_blocks)
    rest = row_blocks * col_blocks
    for pair_idx in range(pairs):
        inner = 4**pair_idx
        outer = span // (4 * inner)
        shaped = tile.reshape(2, outer, 4, inner, outer, 4, inner, rest)
        moved = jnp.transpose(shaped, (0, 2, 5, 1, 3, 4, 6, 7)).reshape(32, -1)
        mixed = jnp.dot(
            kernel, moved, precision=lax.Precision.HIGHEST, preferred_element_type=jnp.float32
        )
        mixed = mixed.reshape(2, 4, 4, outer, inner, outer, inner, rest)
        tile = jnp.transpose(mixed, (0, 3, 1, 4, 5, 2, 6, 7)).reshape(2, span, span, rest)
    tile = tile.reshape(2, span, span, row_blocks, col_blocks)
    return jnp.transpose(tile, (0, 3, 1, 4, 2)).reshape(2, row_count, col_count)


def to_columns(matrix):
    return lax.all_to_all(matrix, HI_GRP, split_axis=2, concat_axis=1, tiled=True)


def to_rows(matrix):
    return cut_exchange(matrix, HI_GRP, 2, 1, 2)


def per_device(rho, perm, superop):
    matrix = rho
    full_order = rho.shape[2]
    layer_count = perm.shape[0]
    for layer_idx in range(layer_count):
        index_table = relabel_table(perm[layer_idx], full_order)
        matrix = jnp.take(matrix, index_table, axis=2)
        matrix = to_columns(matrix)
        matrix = jnp.take(matrix, index_table, axis=1)
        matrix = to_rows(matrix)
        matrix = apply_channel(matrix, superop[layer_idx], PAIRS)
    local_rows = matrix.shape[1]
    position = lax.axis_index(HI_GRP)
    diagonal_block = lax.dynamic_slice_in_dim(matrix[0], position * local_rows, local_rows, 1)
    local_trace = jnp.trace(diagonal_block)
    trace_total = by_axis(local_trace, HI_GRP)
    return (matrix, trace_total / ROWS)


def solution(mesh):
    torus = Mesh(
        mesh.devices.reshape(2, 4, 4, 2, mesh.shape["grp"]), ("hi_0", "hi_1", "hi_2", "hi_3", "grp")
    )
    in_specs = (P(None, HI_GRP, None), P(), P())
    out_specs = (P(None, HI_GRP, None), P())
    return jax.shard_map(
        per_device, mesh=torus, in_specs=in_specs, out_specs=out_specs, check_vma=False
    )
```

profile of v0, /device:TPU:1, one launch (start us, length us, event | category | flops | bytes accessed | tf_op | source)
XLA Modules:
  0.0 1229.9 jit_solution(5795579144434345701)
XLA Ops:
  23.3 59.4 %gather_fusion = f32[8192,2,64]{2,1,0:T(2,128)} fusion(f32[2,64,8192]{1,0,2:T(2,128)} %copy.41, s32[8192]{0:T(1024)S(1)} %broadcast_clamp_fusion.1), kind=kCustom, calls=%fused_computation.clone | custom fusion | bytes 8421376 | tf_op jit(solution)/shard_map/jit(_take)/gather | solution.py:98
  82.7 30.9 %fusion.30 = f32[8192,2,64]{2,1,0:T(2,128)} fusion(f32[8192,2,64]{2,1,0:T(2,128)} %gather_fusion, pred[8192]{0:T(1024)(128)(4,1)S(1)} %compare_and_fusion.1), kind=kLoop, calls=%fused_computation.67 | loop fusion | flops 1048576 | bytes 8396800
  124.7 65.9 %all_to_all.56 = f32[128,1,8192]{2,1,0:T(1,128)} all-to-all(f32[128,1,8192]{2,1,0:T(1,128)} %reshape.283), channel_id=1, replica_groups=mesh['hi_0'=2,'hi_1'=4,'hi_2'=4,'hi_3'=2,'grp'=2] {'hi_0','hi_1','hi_2',..., dimensions={0} | all-to-all | bytes 8388608 | tf_op jit(solution)/shard_map/all_to_all | solution.py:85
  191.1 13.8 %reduce = f32[128,8192]{1,0:T(8,128)} reduce(f32[128,1,8192]{2,1,0:T(1,128)} %all_to_all.56, f32[]{:T(128)} %broadcast.238), dimensions={1}, to_apply=%all_to_all.38.reduce_sub_computation | reduce | bytes 8388612 | tf_op jit(solution)/shard_map/all_to_all | solution.py:85
  239.0 59.4 %gather_fusion.1 = f32[8192,2,64]{2,1,0:T(2,128)} fusion(f32[2,8192,64]{2,0,1:T(2,128)} %bitcast.163, s32[8192]{0:T(1024)S(1)} %broadcast_clamp_fusion.1), kind=kCustom, calls=%fused_computation.1.clone | custom fusion | bytes 8421376 | tf_op jit(solution)/shard_map/jit(_take)/gather | solution.py:100
  298.4 29.5 %broadcast_select_fusion.1 = f32[8192,2,64]{2,1,0:T(2,128)S(1)} fusion(f32[8192,2,64]{2,1,0:T(2,128)} %gather_fusion.1, pred[8192]{0:T(1024)(128)(4,1)S(1)} %compare_and_fusion.1), kind=kLoop, calls=%fused_computation.13 | loop fusion | flops 1048576 | bytes 8396800 | tf_op jit(solution)/shard_map/jit(_take)/select_n | solution.py:100
  350.3 24.1 %all-to-all-done.1 = f32[128,1,4096]{2,1,0:T(1,128)S(1)} async-done(((f32[128,1,4096]{2,1,0:T(1,128)}), f32[128,1,4096]{2,1,0:T(1,128)S(1)}, u32[]{:S(2)}, u32[]{:S(2)}) %all-to-all-start.1) | async-done | bytes 2097184 | tf_op jit(solution)/shard_map/all_to_all | solution.py:35
  433.7 20.6 %reshape_reshape.24 = f32[2,4,16,512,16]{4,3,2,1,0:T(8,128)} reshape(f32[2,64,128,64]{3,2,1,0:T(8,128)} %copy.46) | data formatting | bytes 8388608 | tf_op jit(solution)/shard_map/reshape;reshape | solution.py:67
  454.3 20.5 %copy.47 = f32[2,16,16,4,512]{4,3,2,1,0:T(4,128)} copy(f32[2,16,16,4,512]{2,4,1,3,0:T(8,128)} %bitcast.159) | data formatting | bytes 8388608 | tf_op jit(solution)/shard_map/transpose | solution.py:68
  547.1 27.8 %copy.80 = f32[2,4,16,512,16]{2,1,0,4,3:T(4,128)} copy(f32[2,4,16,512,16]{3,1,4,2,0:T(4,128)} %bitcast.173) | data formatting | bytes 8388608 | tf_op jit(solution)/shard_map/reshape | solution.py:81
  575.0 29.5 %reshape.282 = f32[2,64,8192]{1,0,2:T(2,128)} reshape(f32[2,4,16,512,16]{2,1,0,4,3:T(4,128)} %copy.80) | data formatting | bytes 8388608 | tf_op jit(solution)/shard_map/reshape | solution.py:81
  604.5 59.4 %gather_fusion.2 = f32[8192,2,64]{2,1,0:T(2,128)} fusion(f32[2,64,8192]{1,0,2:T(2,128)} %reshape.282, s32[8192]{0:T(1024)S(1)} %broadcast_clamp_fusion), kind=kCustom, calls=%fused_computation.2.clone | custom fusion | bytes 8421376 | tf_op jit(solution)/shard_map/jit(_take)/gather | solution.py:98
  663.9 30.9 %fusion.31 = f32[8192,2,64]{2,1,0:T(2,128)} fusion(f32[8192,2,64]{2,1,0:T(2,128)} %gather_fusion.2, pred[8192]{0:T(1024)(128)(4,1)S(1)} %compare_and_fusion), kind=kLoop, calls=%fused_computation.68 | loop fusion | flops 1048576 | bytes 8396800
  705.9 60.5 %all_to_all.57 = f32[128,1,8192]{2,1,0:T(1,128)} all-to-all(f32[128,1,8192]{2,1,0:T(1,128)} %reshape.289), channel_id=1, replica_groups=mesh['hi_0'=2,'hi_1'=4,'hi_2'=4,'hi_3'=2,'grp'=2] {'hi_0','hi_1','hi_2',..., dimensions={0} | all-to-all | bytes 8388608 | tf_op jit(solution)/shard_map/all_to_all | solution.py:85
  766.4 13.8 %reduce.3 = f32[128,8192]{1,0:T(8,128)} reduce(f32[128,1,8192]{2,1,0:T(1,128)} %all_to_all.57, f32[]{:T(128)} %broadcast.238), dimensions={1}, to_apply=%all_to_all.44.reduce_sub_computation | reduce | bytes 8388612 | tf_op jit(solution)/shard_map/all_to_all | solution.py:85
  814.3 59.4 %gather_fusion.3 = f32[8192,2,64]{2,1,0:T(2,128)} fusion(f32[2,8192,64]{2,0,1:T(2,128)} %bitcast.165, s32[8192]{0:T(1024)S(1)} %broadcast_clamp_fusion), kind=kCustom, calls=%fused_computation.3.clone | custom fusion | bytes 8421376 | tf_op jit(solution)/shard_map/jit(_take)/gather | solution.py:100
  873.7 29.5 %broadcast_select_fusion = f32[8192,2,64]{2,1,0:T(2,128)S(1)} fusion(f32[8192,2,64]{2,1,0:T(2,128)} %gather_fusion.3, pred[8192]{0:T(1024)(128)(4,1)S(1)} %compare_and_fusion), kind=kLoop, calls=%fused_computation.12 | loop fusion | flops 1048576 | bytes 8396800 | tf_op jit(solution)/shard_map/jit(_take)/select_n | solution.py:100
  925.6 24.1 %all-to-all-done.4 = f32[128,1,4096]{2,1,0:T(1,128)S(1)} async-done(((f32[128,1,4096]{2,1,0:T(1,128)}), f32[128,1,4096]{2,1,0:T(1,128)S(1)}, u32[]{:S(2)}, u32[]{:S(2)}) %all-to-all-start.4) | async-done | bytes 2097184 | tf_op jit(solution)/shard_map/all_to_all | solution.py:35
  966.9 18.7 %all-to-all-done.5 = f32[128,1,4096]{2,1,0:T(1,128)} async-done(((f32[128,1,4096]{2,1,0:T(1,128)}), f32[128,1,4096]{2,1,0:T(1,128)}, u32[]{:S(2)}, u32[]{:S(2)}) %all-to-all-start.5) | async-done | bytes 2097184 | tf_op jit(solution)/shard_map/all_to_all | solution.py:35
  1008.8 20.6 %reshape_reshape.28 = f32[2,4,16,512,16]{4,3,2,1,0:T(8,128)} reshape(f32[2,64,128,64]{3,2,1,0:T(8,128)} %copy.58) | data formatting | bytes 8388608 | tf_op jit(solution)/shard_map/reshape;reshape | solution.py:67
  1029.4 20.5 %copy.59 = f32[2,16,16,4,512]{4,3,2,1,0:T(4,128)} copy(f32[2,16,16,4,512]{2,4,1,3,0:T(8,128)} %bitcast.160) | data formatting | bytes 8388608 | tf_op jit(solution)/shard_map/transpose | solution.py:68
  1132.8 14.2 %squeeze.8 = f32[64,8192]{1,0:T(8,128)S(1)} reshape(f32[1,4,16,512,16]{4,3,2,1,0:T(8,128)} %copy.66) | data formatting | bytes 4194304 | tf_op jit(solution)/shard_map/squeeze | solution.py:105
  1167.9 18.0 %copy.65 = f32[2,4,16,512,16]{4,3,2,1,0:T(8,128)} copy(f32[2,4,16,512,16]{3,1,4,2,0:T(4,128)} %bitcast.172) | data formatting | bytes 8388608 | tf_op jit(solution)/shard_map/transpose | solution.py:81
  1193.7 28.3 %reshape.231 = f32[2,64,8192]{2,1,0:T(8,128)} reshape(f32[2,4,16,512,16]{4,3,2,1,0:T(8,128)} %copy.65) | data formatting | bytes 8388608 | tf_op jit(solution)/shard_map/reshape | solution.py:81
  (88 shorter events, 431.5 us)
Async XLA Ops:
  338.9 35.5 %all-to-all-start.1 = ((f32[128,1,4096]{2,1,0:T(1,128)}), f32[128,1,4096]{2,1,0:T(1,128)S(1)}, u32[]{:S(2)}, u32[]{:S(2)}) async-start(f32[128,1,4096]{2,1,0:T(1,128)} %reshape.287), calls=%async_computation.1 | async-start | bytes 4194304 | tf_op jit(solution)/shard_map/all_to_all | solution.py:35
  344.8 36.6 %copy-start.2 = (f32[2,2,16,16]{3,2,1,0:T(8,128)S(1)}, f32[2,2,16,16]{3,2,1,0:T(8,128)}, u32[]{:S(2)}) copy-start(f32[2,2,16,16]{3,2,1,0:T(8,128)} %param.9) | copy-start | bytes 12292
  374.5 15.4 %copy-start = (f32[128,1,4096]{2,1,0:T(1,128)}, f32[128,1,4096]{2,1,0:T(1,128)S(1)}, u32[]{:S(2)}) copy-start(f32[128,1,4096]{2,1,0:T(1,128)S(1)} %all-to-all-done.1) | copy-start | bytes 6291460
  374.5 36.0 %all-to-all-start.2 = ((f32[128,1,4096]{2,1,0:T(1,128)}), f32[128,1,4096]{2,1,0:T(1,128)}, u32[]{:S(2)}, u32[]{:S(2)}) async-start(f32[128,1,4096]{2,1,0:T(1,128)} %reshape.285), calls=%async_computation.2 | async-start | bytes 4194304 | tf_op jit(solution)/shard_map/all_to_all | solution.py:35
  914.2 35.5 %all-to-all-start.4 = ((f32[128,1,4096]{2,1,0:T(1,128)}), f32[128,1,4096]{2,1,0:T(1,128)S(1)}, u32[]{:S(2)}, u32[]{:S(2)}) async-start(f32[128,1,4096]{2,1,0:T(1,128)} %reshape.293), calls=%async_computation.4 | async-start | bytes 4194304 | tf_op jit(solution)/shard_map/all_to_all | solution.py:35
  949.8 6.9 copy-start.1
  949.8 35.8 %all-to-all-start.5 = ((f32[128,1,4096]{2,1,0:T(1,128)}), f32[128,1,4096]{2,1,0:T(1,128)}, u32[]{:S(2)}, u32[]{:S(2)}) async-start(f32[128,1,4096]{2,1,0:T(1,128)} %reshape.291), calls=%async_computation.5 | async-start | bytes 4194304 | tf_op jit(solution)/shard_map/all_to_all | solution.py:35
where the time goes:
time: 1240 us; the launch traced here: 1230 us
  local copies, waits for them, and re-layouts  722 us (58%)
  other arithmetic  188 us (15%)
  blocking collectives  160 us (13%)
  waiting for transfers between devices  77.3 us (6%)
  matrix products  38.4 us (3%)
  starting transfers between devices  25.3 us (2%)
  between operations  19.1 us (2%)
    all_to_all x2, blocking collectives, to_columns(): lax.all_to_all(matrix, HI_GRP, split_axis=2, concat_axis=1, tiled=True)  126 us
    gather x2, local copies, waits for them, and re-layouts, per_device(): matrix = jnp.take(matrix, index_table, axis=1)  119 us
    gather x2, local copies, waits for them, and re-layouts, per_device(): matrix = jnp.take(matrix, index_table, axis=2)  119 us
    unnamed x19, local copies, waits for them, and re-layouts  86.7 us
    reshape x3, local copies, waits for them, and re-layouts, apply_channel(): return jnp.transpose(tile, (0, 3, 1, 4, 2)).reshape(2, row_count, col_count)  85.7 us
    all_to_all x4, waiting for transfers between devices, cut_exchange(): lax.all_to_all(share, axis, split_axis=0, concat_axis=0, tiled=True)  77.3 us
    unnamed x2, other arithmetic  61.7 us
    select_n x2, other arithmetic, per_device(): matrix = jnp.take(matrix, index_table, axis=1)  59.1 us
  transfers between devices with their start and end apart: 4, of which 4 were waited for; matrix products, arithmetic and copies ran while one was open for 3% of the time, Pallas kernels for 0%

commit v1 on v0

v1 whole, which is shorter than its diff:
```python
import jax
import jax.numpy as jnp
from jax import lax
from jax.experimental import pallas as pl
from jax.experimental.pallas import tpu as pltpu
from jax.sharding import PartitionSpec as P

ROWS = 8192
AX = ("hi", "grp")
RI = 13

W = 0
WINV = 16
U = 32
S0 = 48
A1 = 80
A2 = 112
C2 = 144
P1 = 176
SC = 208
RARE = 220
G = 224
OCCL = 320
OCCT = 328
OCCV = 336
OCCS = 340
TMP = 352
OCC = 384
USED = 400
SIZE = 432


def pick(cond, a, b):
    return jnp.where(cond, jnp.int32(a), jnp.int32(b))


def lane_swaps(T, base, targets, keep, slots, slot0):
    n = len(targets)
    for s in range(16):
        T[TMP + s] = jnp.int32(0)
        T[USED + s] = jnp.int32(0)
    for x in keep:
        T[TMP + x] = jnp.int32(1)
    for k, x in enumerate(targets):
        slot = jnp.int32(-1)
        for s in range(slots):
            slot = pick(T[OCCT + s] == x, s, slot)
        lane = jnp.int32(0)
        for p in range(7):
            lane = pick(T[TMP + T[OCCL + p]] == 0, p, lane)
        active = slot >= 0
        safe = jnp.maximum(slot, 0)
        old = T[OCCL + lane]
        T[OCCL + lane] = jnp.where(active, x, old)
        T[OCCT + safe] = jnp.where(active, old, T[OCCT + safe])
        T[USED + safe] = jnp.where(active, jnp.int32(1), T[USED + safe])
        T[base + 20 + k] = jnp.where(active, jnp.left_shift(jnp.int32(1), lane), 0)
        T[base + k] = slot
    for k in range(n):
        slot = T[base + k]
        free = jnp.int32(0)
        for s in range(slots):
            free = pick(T[USED + s] == 0, s, free)
        slot = jnp.where(slot >= 0, slot, free)
        T[USED + slot] = jnp.int32(1)
        stride = jnp.left_shift(jnp.int32(1), slot + slot0)
        T[base + k] = stride
        T[base + 10 + k] = stride
    for k in range(n, slots):
        free = jnp.int32(0)
        for s in range(slots):
            free = pick(T[USED + s] == 0, s, free)
        T[USED + free] = jnp.int32(1)
        stride = jnp.left_shift(jnp.int32(1), free + slot0)
        T[base + k] = stride
        T[base + 10 + k] = stride


def lane_of(T, x):
    lane = jnp.int32(0)
    for p in range(7):
        lane = pick(T[OCCL + p] == x, p, lane)
    return lane


def matrix_positions(T, base, pair):
    for p in range(7):
        T[TMP + p] = jnp.int32(0)
    for k, x in enumerate((jnp.int32(RI),) + pair):
        lane = lane_of(T, x)
        T[TMP + lane] = jnp.int32(1)
        T[base + k] = lane
    T[base + 3] = jnp.int32(7)
    T[base + 4] = jnp.int32(8)
    for k in range(4):
        free = jnp.int32(0)
        for p in range(7):
            free = pick(T[TMP + p] == 0, p, free)
        T[TMP + free] = jnp.int32(1)
        T[base + 5 + k] = free


def make_plan(perm, T):
    one = jnp.int32(1)
    for q in range(13):
        w = perm[0, perm[1, q]]
        T[W + q] = w
        T[WINV + w] = jnp.int32(q)
    for j in range(4):
        T[U + j] = perm[0, j]
    u = tuple(T[U + j] for j in range(4))
    w = tuple(T[W + q] for q in range(13))
    for p in range(8):
        T[OCCL + p] = jnp.int32(p)
    for s in range(7):
        T[OCCT + s] = jnp.int32(7 + s)
    head = (jnp.int32(RI),) + u
    lane_swaps(T, S0, head, head, 7, 0)
    for k in range(2):
        matrix_positions(T, G + 20 * k, (u[2 * k], u[2 * k + 1]))
    for b in range(16):
        T[TMP + b] = jnp.int32(0)
        T[USED + b] = jnp.int32(0)
    for j in range(4):
        T[TMP + u[j]] = one
    for s in range(10):
        T[OCC + s] = jnp.int32(3 + s)
    for i in range(3):
        mine_u = T[TMP + i]
        mine_ok = jnp.logical_and(mine_u == 0, T[WINV + i] < 6)
        best = jnp.int32(-1)
        spare = jnp.int32(-1)
        for b in range(3, 13):
            free = jnp.logical_and(T[TMP + b] == 0, T[USED + b] == 0)
            spare = pick(free, b, spare)
            best = pick(jnp.logical_and(free, T[WINV + b] < 6), b, best)
        other = jnp.where(mine_u == 0, -1, spare)
        bit = jnp.where(mine_ok, -1, jnp.where(best >= 0, best, other))
        active = bit >= 0
        safe = jnp.maximum(bit, 3)
        T[USED + safe] = jnp.where(active, one, T[USED + safe])
        T[P1 + i] = bit
        T[OCCS + i] = jnp.where(active, bit, jnp.int32(i))
        T[OCC + safe - 3] = jnp.where(active, jnp.int32(i), T[OCC + safe - 3])
        T[P1 + 20 + i] = pick(active, 1 << i, 0)
    T[P1 + 23] = jnp.int32(0)
    T[P1 + 24] = jnp.int32(0)
    for k in range(3):
        bit = T[P1 + k]
        free = jnp.int32(3)
        for b in range(3, 13):
            free = pick(T[USED + b] == 0, b, free)
        bit = jnp.where(bit >= 0, bit, free)
        T[USED + bit] = one
        T[P1 + k] = bit - 3
    for k in range(3, 10):
        free = jnp.int32(3)
        for b in range(3, 13):
            free = pick(T[USED + b] == 0, b, free)
        T[USED + free] = one
        T[P1 + k] = free - 3
    rare = jnp.int32(0)
    rare_amt = jnp.int32(0)
    rare_q = jnp.int32(6)
    for i in range(3):
        q = T[WINV + T[OCCS + i]]
        bad = q >= 6
        rare = pick(bad, 1, rare)
        rare_amt = pick(bad, 1 << i, rare_amt)
        rare_q = jnp.where(bad, q, rare_q)
    other = jnp.int32(0)
    kept = jnp.int32(0)
    rare_bit = jnp.int32(0)
    for s in range(10):
        occ = T[OCC + s]
        in_u = jnp.int32(-1)
        for j in range(4):
            in_u = pick(occ == u[j], 6 + j, in_u)
        place = jnp.where(in_u >= 0, in_u, other)
        other = jnp.where(in_u >= 0, other, other + 1)
        T[TMP + s] = place
        q = T[WINV + occ]
        is_kept = q < 6
        fits = kept < 3
        bit = jnp.where(is_kept, jnp.where(fits, kept, rare_q - 3), q - 3)
        slot = jnp.where(jnp.logical_and(is_kept, fits), kept, 3)
        T[OCCV + slot] = jnp.where(is_kept, occ, jnp.int32(0))
        rare_bit = jnp.where(jnp.logical_and(is_kept, jnp.logical_not(fits)), occ, rare_bit)
        kept = jnp.where(is_kept, kept + 1, kept)
        T[SC + place] = jnp.left_shift(one, bit)
    for i in range(3):
        q = T[WINV + T[OCCS + i]]
        T[OCCS + i] = jnp.where(q >= 6, rare_bit, T[OCCS + i])
    T[RARE] = rare
    T[RARE + 1] = jnp.left_shift(one, rare_q - 3)
    T[RARE + 2] = rare_amt
    for k in range(10):
        s = T[P1 + k]
        T[P1 + k] = jnp.left_shift(one, s)
        T[P1 + 10 + k] = jnp.left_shift(one, T[TMP + s])


def make_plan_2(T):
    one = jnp.int32(1)
    w = tuple(T[W + q] for q in range(13))
    head = w[:5]
    lane_swaps(T, A1, head, head + (jnp.int32(RI),), 7, 3)
    for k in range(3):
        T[A1 + 7 + k] = jnp.int32(1 << k)
        T[A1 + 17 + k] = jnp.int32(1 << k)
    matrix_positions(T, G + 40, (w[0], w[1]))
    for k in range(3):
        T[OCC + k] = 32 + T[OCCV + k]
    for k in range(7):
        T[OCC + 3 + k] = T[OCCT + k]
    for s in range(16):
        T[USED + s] = jnp.int32(0)
    for i in range(3):
        slot = jnp.int32(3)
        for s in range(3, 10):
            good = jnp.logical_and(T[USED + s] == 0, T[WINV + T[OCCT + s - 3]] >= 7)
            slot = pick(good, s, slot)
        T[USED + slot] = one
        T[A2 + i] = slot
        T[A2 + 20 + i] = jnp.int32(1 << i)
        col = T[OCC + slot]
        T[OCC + slot] = 32 + T[OCCS + i]
        T[OCCS + i] = col
    T[A2 + 23] = jnp.int32(0)
    T[A2 + 24] = jnp.int32(0)
    for k in range(3, 10):
        free = jnp.int32(3)
        for s in range(10):
            free = pick(T[USED + s] == 0, s, free)
        T[USED + free] = one
        T[A2 + k] = free
    other = jnp.int32(0)
    for s in range(10):
        occ = T[OCC + s]
        found = jnp.int32(-1)
        for j in range(4):
            found = pick(occ == 32 + w[j], 6 + j, found)
        place = jnp.where(found >= 0, found, other)
        other = jnp.where(found >= 0, other, other + 1)
        T[TMP + s] = place
    for s in range(10):
        T[USED + T[TMP + s]] = T[OCC + s]
    for k in range(10):
        s = T[A2 + k]
        T[A2 + k] = jnp.left_shift(one, s)
        T[A2 + 10 + k] = jnp.left_shift(one, T[TMP + s])
    for s in range(10):
        T[OCC + s] = T[USED + s]
    for i in range(3):
        T[OCC + 6 + i] = T[OCCS + i]
    last = jnp.int32(0)
    for p in range(7):
        x = T[OCCL + p]
        known = x == RI
        for q in range(5):
            known = jnp.logical_or(known, x == w[q])
        last = jnp.where(known, last, x)
    five = last == w[5]
    six = last == w[6]
    ri_lane = pick(five, 6, 5)
    last_lane = pick(five, 5, 6)
    g3 = G + 60
    pos = (jnp.int32(RI), w[2], w[3])
    for k, x in enumerate(pos):
        T[g3 + k] = lane_of(T, x)
    T[g3 + 3] = jnp.int32(7)
    T[g3 + 4] = jnp.int32(8)
    for k, x in enumerate((w[0], w[1], w[4], last)):
        T[g3 + 5 + k] = lane_of(T, x)
    for k, v in enumerate((ri_lane, 2, 3, 7, 8, 0, 1, 4, last_lane)):
        T[g3 + 9 + k] = jnp.int32(v)
    for s in range(10):
        T[USED + s] = jnp.int32(1 if 6 <= s <= 8 else 0)
    lane_swap = []
    for k in range(2):
        slot = jnp.int32(-1)
        for s in range(10):
            slot = pick(T[OCC + s] == w[5 + k], s, slot)
        active = slot >= 0
        safe = jnp.maximum(slot, 0)
        T[USED + safe] = jnp.where(active, one, T[USED + safe])
        T[C2 + 20 + 3 + k] = pick(active, 1 << (5 + k), 0)
        lane_x = jnp.where(ri_lane == 5 + k, jnp.int32(RI), last)
        T[OCC + safe] = jnp.where(active, lane_x, T[OCC + safe])
        lane_swap.append(slot)
    for k in range(2):
        free = jnp.int32(0)
        for s in range(10):
            free = pick(T[USED + s] == 0, s, free)
        slot = jnp.where(lane_swap[k] >= 0, lane_swap[k], free)
        T[USED + slot] = one
        T[C2 + 3 + k] = slot
    for i in range(3):
        T[C2 + i] = jnp.int32(6 + i)
        T[C2 + 20 + i] = jnp.int32(1 << i)
    for k in range(5, 10):
        free = jnp.int32(0)
        for s in range(10):
            free = pick(T[USED + s] == 0, s, free)
        T[USED + free] = one
        T[C2 + k] = free
    for k in range(10):
        s = T[C2 + k]
        occ = T[OCC + s]
        is_row = occ >= 32
        q = T[WINV + jnp.where(is_row, occ - 32, jnp.minimum(occ, 12))]
        bit = jnp.where(is_row, q + 3, q - 7)
        bit = jnp.where(occ == RI, 9, bit)
        T[C2 + k] = jnp.left_shift(one, s)
        T[C2 + 10 + k] = jnp.left_shift(one, bit)


def swap_pass(T, base, kinds, outer, load, store, table_dst=True):
    src = [T[base + k] for k in range(5 + outer)]
    dst = [T[base + 10 + k] for k in range(5 + outer)] if table_dst else src
    amounts = [T[base + 20 + k] for k in range(5)]
    lane = lax.broadcasted_iota(jnp.int32, (8, 128), 1)
    sub = lax.broadcasted_iota(jnp.int32, (8, 128), 0)
    keep_a = []
    keep_b = []
    for k, kind in enumerate(kinds):
        index = lane if kind == "l" else sub
        hit = jnp.bitwise_and(index, amounts[k])
        keep_a.append(hit == 0)
        keep_b.append(hit == amounts[k])

    def offsets(strides):
        offs = [jnp.int32(0)]
        for k in range(5):
            offs = offs + [o + strides[k] for o in offs]
        return offs

    src_offs = offsets(src)
    dst_offs = offsets(dst) if table_dst else src_offs

    def block(b, carry):
        src_base = jnp.int32(0)
        dst_base = jnp.int32(0)
        for k in range(outer):
            bit = jnp.bitwise_and(jnp.right_shift(b, k), 1)
            src_base = src_base + bit * src[5 + k]
            dst_base = dst_base + bit * dst[5 + k]
        if not table_dst:
            dst_base = src_base
        vs = [load(src_base + src_offs[m]) for m in range(32)]
        for k, kind in enumerate(kinds):
            if kind == "l":
                up, down, axis = amounts[k], jnp.bitwise_and(128 - amounts[k], 127), 1
            else:
                up, down, axis = 1 << k, 8 - (1 << k), 0
            for m in range(32):
                if not m >> k & 1:
                    n = m | 1 << k
                    a, b_ = vs[m], vs[n]
                    vs[m] = jnp.where(keep_a[k], a, pltpu.roll(b_, up, axis))
                    vs[n] = jnp.where(keep_b[k], b_, pltpu.roll(a, down, axis))
        for m in range(32):
            store(dst_base + dst_offs[m], vs[m])
        return carry

    lax.fori_loop(0, 1 << outer, block, 0)


def tile_rows(t):
    return pl.ds(pl.multiple_of(t * 8, 8), 8)


def build_matrix(T, base, out_base, sup, gh_ref, gl_ref):
    real, imag = sup[0], sup[1]
    top = jnp.concatenate([real, -imag], axis=1)
    bottom = jnp.concatenate([imag, real], axis=1)
    kern = jnp.concatenate([top, bottom], axis=0)
    index_i = lax.broadcasted_iota(jnp.int32, (512, 32), 0)
    index_o = lax.broadcasted_iota(jnp.int32, (32, 512), 1)

    def code(index, start, first, count):
        total = jnp.zeros_like(index)
        place = {0: 4, 1: 0, 2: 1, 3: 2, 4: 3}
        for k in range(first, first + count):
            bit = jnp.bitwise_and(jnp.right_shift(index, T[start + k]), 1)
            total = total + jnp.left_shift(bit, place[k] if first == 0 else k - first)
        return total

    one_i = (code(index_i, base, 0, 5) == lax.broadcasted_iota(jnp.int32, (512, 32), 1)).astype(jnp.bfloat16)
    one_o = (code(index_o, out_base, 0, 5) == lax.broadcasted_iota(jnp.int32, (32, 512), 0)).astype(jnp.bfloat16)
    rest_i = code(lax.broadcasted_iota(jnp.int32, (512, 128), 0), base, 5, 4)
    rest_o = code(lax.broadcasted_iota(jnp.int32, (8, 512), 1), out_base, 5, 4)
    same = jnp.concatenate([rest_i] * 4, axis=1) == jnp.concatenate([rest_o] * 64, axis=0)
    kh = kern.astype(jnp.bfloat16)
    kl = (kern - kh.astype(jnp.float32)).astype(jnp.bfloat16)
    for part, ref in ((kh, gh_ref), (kl, gl_ref)):
        left = lax.dot_general(one_i, part, (((1,), (1,)), ((), ())), preferred_element_type=jnp.float32)
        full = jnp.dot(left.astype(jnp.bfloat16), one_o, preferred_element_type=jnp.float32)
        ref[...] = jnp.where(same, full, 0.0).astype(jnp.bfloat16)


def mix(parts, gh, gl):
    x = jnp.concatenate(parts, axis=1)
    xh = x.astype(jnp.bfloat16)
    xl = (x - xh.astype(jnp.float32)).astype(jnp.bfloat16)
    y = jnp.dot(xl, gh, preferred_element_type=jnp.float32)
    y = y + jnp.dot(xh, gl, preferred_element_type=jnp.float32)
    return y + jnp.dot(xh, gh, preferred_element_type=jnp.float32)


def split_kernel(perm, rho, out, T):
    @pl.when(pl.program_id(0) == 0)
    def _():
        make_plan(perm, T)
        make_plan_2(T)

    def load(t):
        ri = jnp.right_shift(t, 6)
        ct = jnp.bitwise_and(t, 63)
        return rho[ri, :, pl.ds(pl.multiple_of(ct * 128, 128), 128)]

    def store(t, v):
        out[t] = v

    swap_pass(T, S0, "lllll", 2, load, store, table_dst=False)


def first_kernel(T, sup, x, out, buf, gh0, gl0, gh1, gl1):
    build_matrix(T, G, G, sup, gh0, gl0)
    build_matrix(T, G + 20, G + 20, sup, gh1, gl1)

    def load(t):
        return x[tile_rows(t), :]

    def store(t, v):
        buf[tile_rows(t), :] = v

    swap_pass(T, P1, "sss", 5, load, store)

    def pair0(g, carry):
        rows = [pl.ds(pl.multiple_of((g * 4 + j) * 512, 512), 512) for j in range(4)]
        y = mix([buf[r, :] for r in rows], gh0[...], gl0[...])
        for j in range(4):
            buf[rows[j], :] = y[:, j * 128 : (j + 1) * 128]
        return carry

    lax.fori_loop(0, 4, pair0, 0)
    strides = [T[SC + k] for k in range(10)]
    offs = [jnp.int32(0)]
    for k in range(6):
        offs = offs + [o + strides[k] for o in offs]

    def pair1(h, carry):
        rows = [pl.ds(pl.multiple_of((h + 4 * j) * 512, 512), 512) for j in range(4)]
        y = mix([buf[r, :] for r in rows], gh1[...], gl1[...])
        base = jnp.bitwise_and(h, 1) * strides[6] + jnp.right_shift(h, 1) * strides[7]
        for j in range(4):
            start = base + (strides[8] if j & 1 else 0) + (strides[9] if j & 2 else 0)
            for n in range(64):
                out[tile_rows(start + offs[n]), :] = y[n * 8 : n * 8 + 8, j * 128 : (j + 1) * 128]
        return carry

    lax.fori_loop(0, 4, pair1, 0)

    @pl.when(T[RARE] == 1)
    def _():
        stride = T[RARE + 1]
        amount = T[RARE + 2]
        sub = lax.broadcasted_iota(jnp.int32, (8, 128), 0)
        hit = jnp.bitwise_and(sub, amount)

        def pair(b, carry):
            low = jnp.bitwise_and(b, stride - 1)
            t = (b - low) * 2 + low
            a_rows, b_rows = tile_rows(t), tile_rows(t + stride)
            a, c = out[a_rows, :], out[b_rows, :]
            up = pltpu.roll(c, amount, 0)
            down = pltpu.roll(a, 8 - amount, 0)
            out[a_rows, :] = jnp.where(hit == 0, a, up)
            out[b_rows, :] = jnp.where(hit == amount, c, down)
            return carry

        lax.fori_loop(0, 512, pair, 0)


def second_kernel(T, pos, sup, x, out, trace, buf, buf2, gh0, gl0, gh1, gl1):
    build_matrix(T, G + 40, G + 40, sup, gh0, gl0)
    build_matrix(T, G + 60, G + 69, sup, gh1, gl1)

    def load_x(t):
        return x[tile_rows(t), :]

    def load_1(t):
        return buf[tile_rows(t), :]

    def store_1(t, v):
        buf[tile_rows(t), :] = v

    def load_2(t):
        return buf2[tile_rows(t), :]

    def store_2(t, v):
        buf2[tile_rows(t), :] = v

    swap_pass(T, A1, "lllll", 5, load_x, store_1)
    swap_pass(T, A2, "sss", 5, load_1, store_2)

    def pair0(g, carry):
        rows = [pl.ds(pl.multiple_of((g * 4 + j) * 512, 512), 512) for j in range(4)]
        y = mix([buf2[r, :] for r in rows], gh0[...], gl0[...])
        for j in range(4):
            buf[rows[j], :] = y[:, j * 128 : (j + 1) * 128]
        return carry

    def pair1(h, carry):
        rows = [pl.ds(pl.multiple_of((h + 4 * j) * 512, 512), 512) for j in range(4)]
        y = mix([buf[r, :] for r in rows], gh1[...], gl1[...])
        for j in range(4):
            buf2[rows[j], :] = y[:, j * 128 : (j + 1) * 128]
        return carry

    lax.fori_loop(0, 4, pair0, 0)
    lax.fori_loop(0, 4, pair1, 0)

    def store(t, v):
        ri = jnp.right_shift(t, 9)
        rt = jnp.bitwise_and(jnp.right_shift(t, 6), 7)
        ct = jnp.bitwise_and(t, 63)
        out[ri, tile_rows(rt), pl.ds(pl.multiple_of(ct * 128, 128), 128)] = v

    swap_pass(T, C2, "sssll", 5, load_2, store)
    device = pos[0]
    start = pl.multiple_of(jnp.right_shift(device, 1) * 128, 128)
    block = out[0, :, pl.ds(start, 128)]
    row = lax.broadcasted_iota(jnp.int32, (64, 128), 0) + jnp.bitwise_and(device, 1) * 64
    hit = row == lax.broadcasted_iota(jnp.int32, (64, 128), 1)
    trace[0, 0] = jnp.sum(jnp.where(hit, block, 0.0))


SMEM = pl.BlockSpec(memory_space=pltpu.SMEM)
VMEM = pl.BlockSpec(memory_space=pltpu.VMEM)
MATRICES = [pltpu.VMEM((512, 512), jnp.bfloat16)] * 4
LIMIT = 60 << 20


def exchange(blocks):
    return lax.all_to_all(blocks, AX, split_axis=0, concat_axis=0, tiled=True)


def per_device(rho, perm, superop):
    blocks, table = pl.pallas_call(
        split_kernel,
        grid=(8,),
        in_specs=[SMEM, pl.BlockSpec((2, 8, 8192), lambda i: (0, i, 0))],
        out_specs=[pl.BlockSpec((128, 8, 128), lambda i: (0, i, 0)), SMEM],
        out_shape=[
            jax.ShapeDtypeStruct((128, 64, 128), jnp.float32),
            jax.ShapeDtypeStruct((SIZE,), jnp.int32),
        ],
        name="split",
    )(perm, rho)
    blocks = exchange(blocks)
    blocks = pl.pallas_call(
        first_kernel,
        in_specs=[SMEM, VMEM, VMEM],
        out_specs=VMEM,
        out_shape=jax.ShapeDtypeStruct((8192, 128), jnp.float32),
        scratch_shapes=[pltpu.VMEM((8192, 128), jnp.float32)] + MATRICES,
        compiler_params=pltpu.CompilerParams(vmem_limit_bytes=LIMIT),
        name="first",
    )(table, superop[0], blocks.reshape(8192, 128))
    blocks = exchange(blocks.reshape(128, 64, 128))
    device = lax.axis_index(AX).astype(jnp.int32).reshape(1)
    rho_out, trace = pl.pallas_call(
        second_kernel,
        in_specs=[SMEM, SMEM, VMEM, VMEM],
        out_specs=[VMEM, SMEM],
        out_shape=[
            jax.ShapeDtypeStruct((2, 64, 8192), jnp.float32),
            jax.ShapeDtypeStruct((1, 1), jnp.float32),
        ],
        scratch_shapes=[pltpu.VMEM((8192, 128), jnp.float32)] * 2 + MATRICES,
        compiler_params=pltpu.CompilerParams(vmem_limit_bytes=LIMIT),
        name="second",
    )(table, device, superop[1], blocks.reshape(8192, 128))
    parts = exchange(jnp.broadcast_to(trace[0, 0], (128, 1, 128)))
    return rho_out, jnp.sum(parts[:, 0, 0]) / ROWS


def solution(mesh):
    spec = P(None, AX, None)
    return jax.shard_map(
        per_device, mesh=mesh, in_specs=(spec, P(), P()), out_specs=(spec, P()), check_vma=False
    )
```

time: 1240 us -> 216 us (0.17)
  local copies, waits for them, and re-layouts: 722 us -> 1.26 us
  other arithmetic: 188 us -> 0.73 us
  blocking collectives: 160 us -> 14.8 us
  Pallas kernels: 0 us -> 71.3 us
  matrix products: 38.4 us -> 0 us
  waiting for transfers between devices: 77.3 us -> 107 us
  between operations: 19.1 us -> 2.46 us
    gather x4 -> x0, local copies, waits for them, and re-layouts: 238 us -> none  [the longest x2 119 us: per_device(): matrix = jnp.take(matrix, index_table, axis=1)]
    reshape x9 -> x0, local copies, waits for them, and re-layouts: 113 us -> none  [the longest x3 85.7 us: apply_channel(): return jnp.transpose(tile, (0, 3, 1, 4, 2)).reshape(2, row_count, col_count)]
    all_to_all x2 -> x1, blocking collectives: 126 us -> 14.8 us  [exchange(): return lax.all_to_all(blocks, AX, split_axis=0, concat_axis=0, tiled=True)]
    transpose x11 -> x0, local copies, waits for them, and re-layouts: 105 us -> none  [the longest x2 41.1 us: apply_channel(): jnp.transpose(tile, (0, 2, 4, 1, 3))]
    another operation x18 -> x0, local copies, waits for them, and re-layouts: 92.7 us -> none  [the longest x2 41.3 us: apply_channel(): tile = matrix.reshape(2, row_blocks, span, col_blocks, span)]
    unnamed x19 -> x2, local copies, waits for them, and re-layouts: 86.7 us -> 0.01 us
    pallas_call x0 -> x3, Pallas kernels: none -> 71.3 us  [the longest x1 36.3 us: per_device(): pl.pallas_call(second_kernel, in_specs=[SMEM, SMEM, VMEM, VMEM], out_spec...]
    unnamed x2 -> x0, other arithmetic: 61.7 us -> none
  transfers between devices with their start and end apart: 4 -> 2, of which waited for: 4 -> 2; matrix products, arithmetic and copies ran while one was open for 3% -> 0% of each run, Pallas kernels for 0% -> 0%
where the time goes in v1:
time: 216 us
  waiting for transfers between devices  107 us (50%)
  Pallas kernels  71.3 us (33%)
  starting transfers between devices  17.8 us (8%)
  blocking collectives  14.8 us (7%)
  between operations  2.46 us (1%)
    all_to_all x2, waiting for transfers between devices, exchange(): return lax.all_to_all(blocks, AX, split_axis=0, concat_axis=0, tiled=True)  107 us
    pallas_call x1, Pallas kernels, per_device(): pl.pallas_call(second_kernel, in_specs=[SMEM, SMEM, VMEM, VMEM], out_spec...  36.3 us
    all_to_all x2, starting transfers between devices, exchange(): return lax.all_to_all(blocks, AX, split_axis=0, concat_axis=0, tiled=True)  17.8 us
    pallas_call x1, Pallas kernels, per_device(): pl.pallas_call(split_kernel, grid=(8,), in_specs=[SMEM, pl.BlockSpec((2,...  17.7 us
    pallas_call x1, Pallas kernels, per_device(): pl.pallas_call(first_kernel, in_specs=[SMEM, VMEM, VMEM], out_specs=VMEM,...  17.3 us
    all_to_all x1, blocking collectives, exchange(): return lax.all_to_all(blocks, AX, split_axis=0, concat_axis=0, tiled=True)  14.8 us
  transfers between devices with their start and end apart: 2, of which 2 were waited for; matrix products, arithmetic and copies ran while one was open for 0% of the time, Pallas kernels for 0%

profile of v1, /device:TPU:1, one launch (start us, length us, event | category | flops | bytes accessed | tf_op | source)
XLA Modules:
  0.0 215.8 jit_solution(8518867971202233927)
XLA Ops:
  0.6 17.7 %split.1 = (f32[128,64,128]{2,1,0:T(8,128)}, s32[432]{0:T(512)}) custom-call(s32[2,13]{1,0:T(2,128)} %perm.1, f32[2,64,8192]{2,1,0:T(8,128)} %rho.1), custom_call_target="tpu_custom_call" | custom-call | tf_op jit(solution)/shard_map/split/pallas_call | solution.py:551
  18.4 0.0 copy-start
  18.4 11.9 %all-to-all-start = ((f32[128,64,128]{2,1,0:T(8,128)}), f32[128,64,128]{2,1,0:T(8,128)}, u32[]{:S(2)}, u32[]{:S(2)}) async-start(f32[128,64,128]{2,1,0:T(8,128)} %get-tuple-element.7), calls=%async_computation | async-start | bytes 8388608 | tf_op jit(solution)/shard_map/all_to_all | solution.py:547
  30.3 0.0 copy-done
  30.3 0.6 slice_bitcast_fusion
  30.9 53.4 %all-to-all-done = f32[128,64,128]{2,1,0:T(8,128)} async-done(((f32[128,64,128]{2,1,0:T(8,128)}), f32[128,64,128]{2,1,0:T(8,128)}, u32[]{:S(2)}, u32[]{:S(2)}) %all-to-all-start) | async-done | bytes 4194336 | tf_op jit(solution)/shard_map/all_to_all | solution.py:547
  84.3 17.3 %first.1 = f32[8192,128]{1,0:T(8,128)} custom-call(s32[432]{0:T(512)} %get-tuple-element.6.T, f32[2,16,16]{2,1,0:T(8,128)} %get-tuple-element.10.sup, f32[8192,128]{1,0:T(8,128)} %bitcast.3.x), custom_call_target="tpu_custom_call" | custom-call | tf_op jit(solution)/shard_map/first/pallas_call | solution.py:563
  101.6 5.8 %all-to-all-start.1 = ((f32[128,64,128]{2,1,0:T(8,128)}), f32[128,64,128]{2,1,0:T(8,128)}, u32[]{:S(2)}, u32[]{:S(2)}) async-start(f32[128,64,128]{2,1,0:T(8,128)} %bitcast.9), calls=%async_computation.1 | async-start | bytes 8388608 | tf_op jit(solution)/shard_map/all_to_all | solution.py:547
  107.5 54.0 %all-to-all-done.1 = f32[128,64,128]{2,1,0:T(8,128)} async-done(((f32[128,64,128]{2,1,0:T(8,128)}), f32[128,64,128]{2,1,0:T(8,128)}, u32[]{:S(2)}, u32[]{:S(2)}) %all-to-all-start.1) | async-done | bytes 4194336 | tf_op jit(solution)/shard_map/all_to_all | solution.py:547
  161.5 36.3 %second.1 = (f32[2,64,8192]{2,1,0:T(8,128)}, f32[1,1]{1,0:T(1,128)}) custom-call(s32[432]{0:T(512)} %get-tuple-element.6.T, s32[1]{0:T(128)} %bitcast.pos, f32[2,16,16]{2,1,0:T(8,128)} %get-tuple-element.11.sup, f32[8192,128]{1,0:T(8,128)} %bitcast.5.x), custom_call_target="tpu_custom_call" | custom-call | tf_op jit(solution)/shard_map/second/pallas_call | solution.py:574
  197.8 0.6 broadcast_in_dim.3
  198.5 14.8 %all_to_all.15 = f32[128,1,128]{2,1,0:T(1,128)S(1)} all-to-all(f32[128,1,128]{2,1,0:T(1,128)S(1)} %broadcast_in_dim.3), channel_id=1, replica_groups=mesh['hi'=64,'grp'=2] {'hi','grp'}, dimensions={0} | all-to-all | bytes 131072 | tf_op jit(solution)/shard_map/all_to_all | solution.py:547
  213.3 0.7 slice_reduce_fusion
Async XLA Ops:
  18.4 12.0 %copy-start = (f32[2,2,16,16]{3,2,1,0:T(8,128)S(1)}, f32[2,2,16,16]{3,2,1,0:T(8,128)}, u32[]{:S(2)}) copy-start(f32[2,2,16,16]{3,2,1,0:T(8,128)} %param.5) | copy-start | bytes 12292
  18.4 66.0 %all-to-all-start = ((f32[128,64,128]{2,1,0:T(8,128)}), f32[128,64,128]{2,1,0:T(8,128)}, u32[]{:S(2)}, u32[]{:S(2)}) async-start(f32[128,64,128]{2,1,0:T(8,128)} %get-tuple-element.7), calls=%async_computation | async-start | bytes 8388608 | tf_op jit(solution)/shard_map/all_to_all | solution.py:547
  101.6 59.9 %all-to-all-start.1 = ((f32[128,64,128]{2,1,0:T(8,128)}), f32[128,64,128]{2,1,0:T(8,128)}, u32[]{:S(2)}, u32[]{:S(2)}) async-start(f32[128,64,128]{2,1,0:T(8,128)} %bitcast.9), calls=%async_computation.1 | async-start | bytes 8388608 | tf_op jit(solution)/shard_map/all_to_all | solution.py:547

commit v2 on v1

--- a/solution.py
+++ b/solution.py
@@ -100,8 +100,7 @@
         T[base + 5 + k] = free
 
 
-def make_plan(perm, T):
-    one = jnp.int32(1)
+def make_plan_0(perm, T):
     for q in range(13):
         w = perm[0, perm[1, q]]
         T[W + q] = w
@@ -109,13 +108,17 @@
     for j in range(4):
         T[U + j] = perm[0, j]
     u = tuple(T[U + j] for j in range(4))
-    w = tuple(T[W + q] for q in range(13))
     for p in range(8):
         T[OCCL + p] = jnp.int32(p)
     for s in range(7):
         T[OCCT + s] = jnp.int32(7 + s)
     head = (jnp.int32(RI),) + u
     lane_swaps(T, S0, head, head, 7, 0)
+
+
+def make_plan_1(T):
+    one = jnp.int32(1)
+    u = tuple(T[U + j] for j in range(4))
     for k in range(2):
         matrix_positions(T, G + 20 * k, (u[2 * k], u[2 * k + 1]))
     for b in range(16):
@@ -315,28 +318,31 @@
         T[C2 + 10 + k] = jnp.left_shift(one, bit)
 
 
-def swap_pass(T, base, kinds, outer, load, store, table_dst=True):
-    src = [T[base + k] for k in range(5 + outer)]
-    dst = [T[base + 10 + k] for k in range(5 + outer)] if table_dst else src
+def swap_pass(T, base, kinds, outer, load, store, src=None):
+    if src is None:
+        src = [T[base + k] * 8 for k in range(5 + outer)]
+    dst = [T[base + 10 + k] * 8 for k in range(5 + outer)]
     amounts = [T[base + 20 + k] for k in range(5)]
     lane = lax.broadcasted_iota(jnp.int32, (8, 128), 1)
     sub = lax.broadcasted_iota(jnp.int32, (8, 128), 0)
     keep_a = []
     keep_b = []
+    partner = []
     for k, kind in enumerate(kinds):
         index = lane if kind == "l" else sub
         hit = jnp.bitwise_and(index, amounts[k])
         keep_a.append(hit == 0)
         keep_b.append(hit == amounts[k])
-
-    def offsets(strides):
-        offs = [jnp.int32(0)]
-        for k in range(5):
-            offs = offs + [o + strides[k] for o in offs]
-        return offs
-
-    src_offs = offsets(src)
-    dst_offs = offsets(dst) if table_dst else src_offs
+        partner.append(jnp.bitwise_xor(lane, amounts[k]))
+
+    def sums(start, strides):
+        out = [start]
+        for stride in strides:
+            out = out + [o + stride for o in out]
+        return out
+
+    src_low = sums(jnp.int32(0), src[:3])
+    dst_low = sums(jnp.int32(0), dst[:3])
 
     def block(b, carry):
         src_base = jnp.int32(0)
@@ -345,29 +351,34 @@
             bit = jnp.bitwise_and(jnp.right_shift(b, k), 1)
             src_base = src_base + bit * src[5 + k]
             dst_base = dst_base + bit * dst[5 + k]
-        if not table_dst:
-            dst_base = src_base
-        vs = [load(src_base + src_offs[m]) for m in range(32)]
+        vs = []
+        for high in sums(src_base, src[3:5]):
+            vs.extend(load(high + low, n) for n, low in enumerate(src_low))
         for k, kind in enumerate(kinds):
-            if kind == "l":
-                up, down, axis = amounts[k], jnp.bitwise_and(128 - amounts[k], 127), 1
-            else:
-                up, down, axis = 1 << k, 8 - (1 << k), 0
             for m in range(32):
                 if not m >> k & 1:
                     n = m | 1 << k
-                    a, b_ = vs[m], vs[n]
-                    vs[m] = jnp.where(keep_a[k], a, pltpu.roll(b_, up, axis))
-                    vs[n] = jnp.where(keep_b[k], b_, pltpu.roll(a, down, axis))
-        for m in range(32):
-            store(dst_base + dst_offs[m], vs[m])
+                    x, y = vs[m], vs[n]
+                    if kind == "l":
+                        moved = jnp.where(keep_a[k], y, x)
+                        moved = jnp.take_along_axis(moved, partner[k], axis=1, mode="promise_in_bounds")
+                        vs[m] = jnp.where(keep_a[k], x, moved)
+                        vs[n] = jnp.where(keep_b[k], y, moved)
+                    else:
+                        vs[m] = jnp.where(keep_a[k], x, pltpu.roll(y, 1 << k, 0))
+                        vs[n] = jnp.where(keep_b[k], y, pltpu.roll(x, 8 - (1 << k), 0))
+        m = 0
+        for high in sums(dst_base, dst[3:5]):
+            for low in dst_low:
+                store(high + low, vs[m])
+                m += 1
         return carry
 
     lax.fori_loop(0, 1 << outer, block, 0)
 
 
-def tile_rows(t):
-    return pl.ds(pl.multiple_of(t * 8, 8), 8)
+def tile_rows(row):
+    return pl.ds(pl.multiple_of(row, 8), 8)
 
 
 def build_matrix(T, base, out_base, sup, gh_ref, gl_ref):
@@ -411,56 +422,83 @@
 def split_kernel(perm, rho, out, T):
     @pl.when(pl.program_id(0) == 0)
     def _():
-        make_plan(perm, T)
-        make_plan_2(T)
-
-    def load(t):
-        ri = jnp.right_shift(t, 6)
-        ct = jnp.bitwise_and(t, 63)
-        return rho[ri, :, pl.ds(pl.multiple_of(ct * 128, 128), 128)]
-
-    def store(t, v):
-        out[t] = v
-
-    swap_pass(T, S0, "lllll", 2, load, store, table_dst=False)
-
-
-def first_kernel(T, sup, x, out, buf, gh0, gl0, gh1, gl1):
-    build_matrix(T, G, G, sup, gh0, gl0)
-    build_matrix(T, G + 20, G + 20, sup, gh1, gl1)
-
-    def load(t):
-        return x[tile_rows(t), :]
-
-    def store(t, v):
-        buf[tile_rows(t), :] = v
-
-    swap_pass(T, P1, "sss", 5, load, store)
-
-    def pair0(g, carry):
-        rows = [pl.ds(pl.multiple_of((g * 4 + j) * 512, 512), 512) for j in range(4)]
-        y = mix([buf[r, :] for r in rows], gh0[...], gl0[...])
+        make_plan_0(perm, T)
+
+    rows = out.reshape(1024, 128)
+
+    def load(lane, n):
+        return rho[n & 1, :, pl.ds(pl.multiple_of(lane, 128), 128)]
+
+    def store(row, v):
+        rows[tile_rows(row), :] = v
+
+    src = [jnp.int32(0)] + [T[S0 + k] * 128 for k in range(1, 7)]
+    swap_pass(T, S0, "lllll", 2, load, store, src)
+
+
+def prepare_kernel(first_table, sup, T, matrices):
+    def copy(k, carry):
+        T[k] = first_table[k]
+        return carry
+
+    lax.fori_loop(0, TMP, copy, 0)
+    make_plan_1(T)
+    make_plan_2(T)
+    for k, (base, out_base) in enumerate(((G, G), (G + 20, G + 20), (G + 40, G + 40), (G + 60, G + 69))):
+        build_matrix(T, base, out_base, sup[k // 2], matrices.at[2 * k], matrices.at[2 * k + 1])
+
+
+def reader(ref):
+    return lambda row, n: ref[tile_rows(row), :]
+
+
+def writer(ref):
+    def store(row, v):
+        ref[tile_rows(row), :] = v
+
+    return store
+
+
+def mix_pass(src, dst, matrices, step, store=None):
+    def body(g, carry):
+        first = g * 4 if step == 1 else g
+        rows = [pl.ds(pl.multiple_of((first + step * j) * 512, 512), 512) for j in range(4)]
+        y = mix([src[r, :] for r in rows], matrices[0], matrices[1])
         for j in range(4):
-            buf[rows[j], :] = y[:, j * 128 : (j + 1) * 128]
+            piece = y[:, j * 128 : (j + 1) * 128]
+            if store is None:
+                dst[rows[j], :] = piece
+            else:
+                store(g, j, piece)
         return carry
 
-    lax.fori_loop(0, 4, pair0, 0)
-    strides = [T[SC + k] for k in range(10)]
-    offs = [jnp.int32(0)]
-    for k in range(6):
-        offs = offs + [o + strides[k] for o in offs]
-
-    def pair1(h, carry):
-        rows = [pl.ds(pl.multiple_of((h + 4 * j) * 512, 512), 512) for j in range(4)]
-        y = mix([buf[r, :] for r in rows], gh1[...], gl1[...])
-        base = jnp.bitwise_and(h, 1) * strides[6] + jnp.right_shift(h, 1) * strides[7]
-        for j in range(4):
-            start = base + (strides[8] if j & 1 else 0) + (strides[9] if j & 2 else 0)
-            for n in range(64):
-                out[tile_rows(start + offs[n]), :] = y[n * 8 : n * 8 + 8, j * 128 : (j + 1) * 128]
-        return carry
-
-    lax.fori_loop(0, 4, pair1, 0)
+    lax.fori_loop(0, 4, body, 0)
+
+
+def first_kernel(T, matrices_hbm, x, out, buf, matrices, sem):
+    fetch = pltpu.make_async_copy(matrices_hbm.at[pl.ds(0, 4)], matrices, sem)
+    fetch.start()
+    swap_pass(T, P1, "sss", 5, reader(x), writer(buf))
+    fetch.wait()
+    mix_pass(buf, buf, matrices.at[pl.ds(0, 2)], 1)
+    strides = [T[SC + k] * 8 for k in range(10)]
+    low = [jnp.int32(0)]
+    for k in range(3):
+        low = low + [o + strides[k] for o in low]
+
+    def scatter(h, j, piece):
+        start = jnp.bitwise_and(h, 1) * strides[6] + jnp.right_shift(h, 1) * strides[7]
+        if j & 1:
+            start = start + strides[8]
+        if j & 2:
+            start = start + strides[9]
+        high = [start]
+        for k in range(3, 6):
+            high = high + [o + strides[k] for o in high]
+        for n in range(64):
+            out[tile_rows(high[n >> 3] + low[n & 7]), :] = piece[n * 8 : n * 8 + 8, :]
+
+    mix_pass(buf, None, matrices.at[pl.ds(2, 2)], 4, scatter)
 
     @pl.when(T[RARE] == 1)
     def _():
@@ -472,7 +510,7 @@
         def pair(b, carry):
             low = jnp.bitwise_and(b, stride - 1)
             t = (b - low) * 2 + low
-            a_rows, b_rows = tile_rows(t), tile_rows(t + stride)
+            a_rows, b_rows = tile_rows(t * 8), tile_rows((t + stride) * 8)
             a, c = out[a_rows, :], out[b_rows, :]
             up = pltpu.roll(c, amount, 0)
             down = pltpu.roll(a, 8 - amount, 0)
@@ -483,64 +521,33 @@
         lax.fori_loop(0, 512, pair, 0)
 
 
-def second_kernel(T, pos, sup, x, out, trace, buf, buf2, gh0, gl0, gh1, gl1):
-    build_matrix(T, G + 40, G + 40, sup, gh0, gl0)
-    build_matrix(T, G + 60, G + 69, sup, gh1, gl1)
-
-    def load_x(t):
-        return x[tile_rows(t), :]
-
-    def load_1(t):
-        return buf[tile_rows(t), :]
-
-    def store_1(t, v):
-        buf[tile_rows(t), :] = v
-
-    def load_2(t):
-        return buf2[tile_rows(t), :]
-
-    def store_2(t, v):
-        buf2[tile_rows(t), :] = v
-
-    swap_pass(T, A1, "lllll", 5, load_x, store_1)
-    swap_pass(T, A2, "sss", 5, load_1, store_2)
-
-    def pair0(g, carry):
-        rows = [pl.ds(pl.multiple_of((g * 4 + j) * 512, 512), 512) for j in range(4)]
-        y = mix([buf2[r, :] for r in rows], gh0[...], gl0[...])
-        for j in range(4):
-            buf[rows[j], :] = y[:, j * 128 : (j + 1) * 128]
-        return carry
-
-    def pair1(h, carry):
-        rows = [pl.ds(pl.multiple_of((h + 4 * j) * 512, 512), 512) for j in range(4)]
-        y = mix([buf[r, :] for r in rows], gh1[...], gl1[...])
-        for j in range(4):
-            buf2[rows[j], :] = y[:, j * 128 : (j + 1) * 128]
-        return carry
-
-    lax.fori_loop(0, 4, pair0, 0)
-    lax.fori_loop(0, 4, pair1, 0)
-
-    def store(t, v):
-        ri = jnp.right_shift(t, 9)
-        rt = jnp.bitwise_and(jnp.right_shift(t, 6), 7)
-        ct = jnp.bitwise_and(t, 63)
-        out[ri, tile_rows(rt), pl.ds(pl.multiple_of(ct * 128, 128), 128)] = v
-
-    swap_pass(T, C2, "sssll", 5, load_2, store)
+def second_kernel(T, pos, matrices_hbm, x, out, trace, buf, buf2, matrices, sem):
+    fetch = pltpu.make_async_copy(matrices_hbm.at[pl.ds(4, 4)], matrices, sem)
+    fetch.start()
+    swap_pass(T, A1, "lllll", 5, reader(x), writer(buf))
+    swap_pass(T, A2, "sss", 5, reader(buf), writer(buf2))
+    fetch.wait()
+    mix_pass(buf2, buf, matrices.at[pl.ds(0, 2)], 1)
+    mix_pass(buf, buf2, matrices.at[pl.ds(2, 2)], 4)
+    swap_pass(T, C2, "sssll", 5, reader(buf2), writer(out))
     device = pos[0]
-    start = pl.multiple_of(jnp.right_shift(device, 1) * 128, 128)
-    block = out[0, :, pl.ds(start, 128)]
-    row = lax.broadcasted_iota(jnp.int32, (64, 128), 0) + jnp.bitwise_and(device, 1) * 64
-    hit = row == lax.broadcasted_iota(jnp.int32, (64, 128), 1)
-    trace[0, 0] = jnp.sum(jnp.where(hit, block, 0.0))
+    column = jnp.right_shift(device, 1)
+    shift = jnp.bitwise_and(device, 1) * 64
+    sub = lax.broadcasted_iota(jnp.int32, (8, 128), 0)
+    lane = lax.broadcasted_iota(jnp.int32, (8, 128), 1)
+    total = jnp.zeros((8, 128), jnp.float32)
+    for t in range(8):
+        tile = out[tile_rows((t * 64 + column) * 8), :]
+        total = total + jnp.where(lane == sub + (t * 8 + shift), tile, 0.0)
+    trace[0, 0] = jnp.sum(total)
 
 
 SMEM = pl.BlockSpec(memory_space=pltpu.SMEM)
 VMEM = pl.BlockSpec(memory_space=pltpu.VMEM)
-MATRICES = [pltpu.VMEM((512, 512), jnp.bfloat16)] * 4
+HBM = pl.BlockSpec(memory_space=pl.ANY)
 LIMIT = 60 << 20
+BUFFER = pltpu.VMEM((8192, 128), jnp.float32)
+MATRICES = pltpu.VMEM((4, 512, 512), jnp.bfloat16)
 
 
 def exchange(blocks):
@@ -559,30 +566,42 @@
         ],
         name="split",
     )(perm, rho)
+    table, matrices = pl.pallas_call(
+        prepare_kernel,
+        in_specs=[SMEM, VMEM],
+        out_specs=[SMEM, VMEM],
+        out_shape=[
+            jax.ShapeDtypeStruct((SIZE,), jnp.int32),
+            jax.ShapeDtypeStruct((8, 512, 512), jnp.bfloat16),
+        ],
+        compiler_params=pltpu.CompilerParams(vmem_limit_bytes=LIMIT),
+        name="prepare",
+    )(table, superop)
     blocks = exchange(blocks)
     blocks = pl.pallas_call(
         first_kernel,
-        in_specs=[SMEM, VMEM, VMEM],
+        in_specs=[SMEM, HBM, VMEM],
         out_specs=VMEM,
         out_shape=jax.ShapeDtypeStruct((8192, 128), jnp.float32),
-        scratch_shapes=[pltpu.VMEM((8192, 128), jnp.float32)] + MATRICES,
+        scratch_shapes=[BUFFER, MATRICES, pltpu.SemaphoreType.DMA],
         compiler_params=pltpu.CompilerParams(vmem_limit_bytes=LIMIT),
         name="first",
-    )(table, superop[0], blocks.reshape(8192, 128))
+    )(table, matrices, blocks.reshape(8192, 128))
     blocks = exchange(blocks.reshape(128, 64, 128))
     device = lax.axis_index(AX).astype(jnp.int32).reshape(1)
-    rho_out, trace = pl.pallas_call(
+    tiles, trace = pl.pallas_call(
         second_kernel,
-        in_specs=[SMEM, SMEM, VMEM, VMEM],
+        in_specs=[SMEM, SMEM, HBM, VMEM],
         out_specs=[VMEM, SMEM],
         out_shape=[
-            jax.ShapeDtypeStruct((2, 64, 8192), jnp.float32),
+            jax.ShapeDtypeStruct((8192, 128), jnp.float32),
             jax.ShapeDtypeStruct((1, 1), jnp.float32),
         ],
-        scratch_shapes=[pltpu.VMEM((8192, 128), jnp.float32)] * 2 + MATRICES,
+        scratch_shapes=[BUFFER, BUFFER, MATRICES, pltpu.SemaphoreType.DMA],
         compiler_params=pltpu.CompilerParams(vmem_limit_bytes=LIMIT),
         name="second",
-    )(table, device, superop[1], blocks.reshape(8192, 128))
+    )(table, device, matrices, blocks.reshape(8192, 128))
+    rho_out = tiles.reshape(2, 8, 64, 8, 128).transpose(0, 1, 3, 2, 4).reshape(2, 64, 8192)
     parts = exchange(jnp.broadcast_to(trace[0, 0], (128, 1, 128)))
     return rho_out, jnp.sum(parts[:, 0, 0]) / ROWS
 

time: 216 us -> 208 us (0.963)
  waiting for transfers between devices: 107 us -> 98.9 us
    all_to_all x2, waiting for transfers between devices: 107 us -> 98.9 us  [exchange(): return lax.all_to_all(blocks, AX, split_axis=0, concat_axis=0, tiled=True)]
    pallas_call x2 -> x3, Pallas kernels: 53.6 us -> 56.9 us  [the longest x1 33.4 us: per_device(): pl.pallas_call(second_kernel, in_specs=[SMEM, SMEM, HBM, VMEM], out_specs...]
    pallas_call x1, Pallas kernels: 17.7 us -> 15.4 us  [per_device(): pl.pallas_call(split_kernel, grid=(8,), in_specs=[SMEM, pl.BlockSpec((2,...]
  transfers between devices with their start and end apart: 2 -> 2, of which waited for: 2 -> 2; matrix products, arithmetic and copies ran while one was open for 0% -> 0% of each run, Pallas kernels for 0% -> 4%
where the time goes in v2:
time: 208 us
  waiting for transfers between devices  98.9 us (48%)
  Pallas kernels  72.3 us (35%)
  starting transfers between devices  17.8 us (9%)
  blocking collectives  14.8 us (7%)
  between operations  2.46 us (1%)
    all_to_all x2, waiting for transfers between devices, exchange(): return lax.all_to_all(blocks, AX, split_axis=0, concat_axis=0, tiled=True)  98.9 us
    pallas_call x1, Pallas kernels, per_device(): pl.pallas_call(second_kernel, in_specs=[SMEM, SMEM, HBM, VMEM], out_specs...  33.4 us
    all_to_all x2, starting transfers between devices, exchange(): return lax.all_to_all(blocks, AX, split_axis=0, concat_axis=0, tiled=True)  17.8 us
    pallas_call x1, Pallas kernels, per_device(): pl.pallas_call(split_kernel, grid=(8,), in_specs=[SMEM, pl.BlockSpec((2,...  15.4 us
    all_to_all x1, blocking collectives, exchange(): return lax.all_to_all(blocks, AX, split_axis=0, concat_axis=0, tiled=True)  14.8 us
    pallas_call x1, Pallas kernels, per_device(): pl.pallas_call(first_kernel, in_specs=[SMEM, HBM, VMEM], out_specs=VMEM,...  14.4 us
    pallas_call x1, Pallas kernels, per_device(): pl.pallas_call(prepare_kernel, in_specs=[SMEM, VMEM], out_specs=[SMEM, VM...  9.12 us
  transfers between devices with their start and end apart: 2, of which 2 were waited for; matrix products, arithmetic and copies ran while one was open for 0% of the time, Pallas kernels for 4%

profile of v2, /device:TPU:1, one launch (start us, length us, event | category | flops | bytes accessed | tf_op | source)
XLA Modules:
  0.0 207.7 jit_solution(3432159356745291201)
XLA Ops:
  0.6 15.4 %split.1 = (f32[128,64,128]{2,1,0:T(8,128)}, s32[432]{0:T(512)}) custom-call(s32[2,13]{1,0:T(2,128)} %perm.1, f32[2,64,8192]{2,1,0:T(8,128)} %rho.1), custom_call_target="tpu_custom_call" | custom-call | tf_op jit(solution)/shard_map/split/pallas_call | solution.py:558
  16.1 11.9 %all-to-all-start = ((f32[128,64,128]{2,1,0:T(8,128)}), f32[128,64,128]{2,1,0:T(8,128)}, u32[]{:S(2)}, u32[]{:S(2)}) async-start(f32[128,64,128]{2,1,0:T(8,128)} %get-tuple-element.11), calls=%async_computation | async-start | bytes 8388608 | tf_op jit(solution)/shard_map/all_to_all | solution.py:554
  28.0 9.1 %prepare.1 = (s32[432]{0:T(512)}, bf16[8,512,512]{2,1,0:T(8,128)(2,1)}) custom-call(s32[432]{0:T(512)} %get-tuple-element.8.first_table, f32[2,2,16,16]{3,2,1,0:T(8,128)} %sup.1), custom_call_target="tpu_custom_call" | custom-call | tf_op jit(solution)/shard_map/prepare/pallas_call | solution.py:569
  37.1 44.9 %all-to-all-done = f32[128,64,128]{2,1,0:T(8,128)} async-done(((f32[128,64,128]{2,1,0:T(8,128)}), f32[128,64,128]{2,1,0:T(8,128)}, u32[]{:S(2)}, u32[]{:S(2)}) %all-to-all-start) | async-done | bytes 4194336 | tf_op jit(solution)/shard_map/all_to_all | solution.py:554
  82.0 14.4 %first.1 = f32[8192,128]{1,0:T(8,128)} custom-call(s32[432]{0:T(512)} %get-tuple-element.9.T, bf16[8,512,512]{2,1,0:T(8,128)(2,1)} %get-tuple-element.10.matrices_hbm, f32[8192,128]{1,0:T(8,128)} %bitcast.1.x), custom_call_target="tpu_custom_call" | custom-call | tf_op jit(solution)/shard_map/first/pallas_call | solution.py:581
  96.4 5.9 %all-to-all-start.1 = ((f32[128,64,128]{2,1,0:T(8,128)}), f32[128,64,128]{2,1,0:T(8,128)}, u32[]{:S(2)}, u32[]{:S(2)}) async-start(f32[128,64,128]{2,1,0:T(8,128)} %bitcast.10), calls=%async_computation.1 | async-start | bytes 8388608 | tf_op jit(solution)/shard_map/all_to_all | solution.py:554
  102.3 54.0 %all-to-all-done.1 = f32[128,64,128]{2,1,0:T(8,128)} async-done(((f32[128,64,128]{2,1,0:T(8,128)}), f32[128,64,128]{2,1,0:T(8,128)}, u32[]{:S(2)}, u32[]{:S(2)}) %all-to-all-start.1) | async-done | bytes 4194336 | tf_op jit(solution)/shard_map/all_to_all | solution.py:554
  156.3 33.4 %second.1 = (f32[8192,128]{1,0:T(8,128)}, f32[1,1]{1,0:T(1,128)}) custom-call(s32[432]{0:T(512)} %get-tuple-element.9.T, s32[1]{0:T(128)} %bitcast.pos, bf16[8,512,512]{2,1,0:T(8,128)(2,1)} %get-tuple-element.10.matrices_hbm, f32[8192,128]{1,0:T(8,128)} %bitcast.3.x), custom_call_target="tpu_custom_call" | custom-call | tf_op jit(solution)/shard_map/second/pallas_call | solution.py:592
  189.7 0.7 broadcast_in_dim.3
  190.3 14.8 %all_to_all.15 = f32[128,1,128]{2,1,0:T(1,128)S(1)} all-to-all(f32[128,1,128]{2,1,0:T(1,128)S(1)} %broadcast_in_dim.3), channel_id=1, replica_groups=mesh['hi'=64,'grp'=2] {'hi','grp'}, dimensions={0} | all-to-all | bytes 131072 | tf_op jit(solution)/shard_map/all_to_all | solution.py:554
  205.2 0.7 slice_reduce_fusion
Async XLA Ops:
  16.1 66.0 %all-to-all-start = ((f32[128,64,128]{2,1,0:T(8,128)}), f32[128,64,128]{2,1,0:T(8,128)}, u32[]{:S(2)}, u32[]{:S(2)}) async-start(f32[128,64,128]{2,1,0:T(8,128)} %get-tuple-element.11), calls=%async_computation | async-start | bytes 8388608 | tf_op jit(solution)/shard_map/all_to_all | solution.py:554
  96.4 59.9 %all-to-all-start.1 = ((f32[128,64,128]{2,1,0:T(8,128)}), f32[128,64,128]{2,1,0:T(8,128)}, u32[]{:S(2)}, u32[]{:S(2)}) async-start(f32[128,64,128]{2,1,0:T(8,128)} %bitcast.10), calls=%async_computation.1 | async-start | bytes 8388608 | tf_op jit(solution)/shard_map/all_to_all | solution.py:554

commit v3 on v2

v3 whole, which is shorter than its diff:
```python
import jax
import jax.numpy as jnp
from jax import lax
from jax.experimental import pallas as pl
from jax.experimental.pallas import tpu as pltpu
from jax.sharding import PartitionSpec as P

ROWS = 8192
AX = ("hi", "grp")
RI = 13

W = 0
WINV = 16
U = 32
S0 = 48
A2 = 80
C2 = 112
P1 = 176
SC = 208
RARE = 220
G = 224
OCCL = 320
OCCT = 328
OCCR = 336
SUBC = 344
TMP = 352
OCC = 384
USED = 400
SIZE = 432


def pick(cond, a, b):
    return jnp.where(cond, jnp.int32(a), jnp.int32(b))


def lane_of(T, lanes, x):
    lane = jnp.int32(0)
    for p in range(7):
        lane = pick(T[lanes + p] == x, p, lane)
    return lane


def other_lanes(T, base, taken):
    for p in range(7):
        T[TMP + p] = jnp.int32(0)
    for lane in taken:
        T[TMP + lane] = jnp.int32(1)
    for k in range(4):
        free = jnp.int32(0)
        for p in range(7):
            free = pick(T[TMP + p] == 0, p, free)
        T[TMP + free] = jnp.int32(1)
        T[base + 5 + k] = free


def fill_slots(T, base, done, slots=10):
    for k in range(slots):
        free = jnp.int32(0)
        for s in range(slots):
            free = pick(T[USED + s] == 0, s, free)
        if k < done:
            free = jnp.where(T[base + k] >= 0, T[base + k], free)
        T[USED + free] = jnp.int32(1)
        T[base + k] = free


def set_strides(T, base, target):
    for k in range(10):
        s = T[base + k]
        T[base + k] = jnp.left_shift(jnp.int32(1), s)
        T[base + 10 + k] = jnp.left_shift(jnp.int32(1), T[target + s])


def make_plan_0(perm, T):
    one = jnp.int32(1)
    for q in range(13):
        w = perm[0, perm[1, q]]
        T[W + q] = w
        T[WINV + w] = jnp.int32(q)
    for b in range(16):
        T[TMP + b] = jnp.int32(0)
        T[USED + b] = jnp.int32(0)
    for q in range(4):
        T[TMP + T[W + q]] = jnp.int32(2)
    for j in range(4):
        T[U + j] = perm[0, j]
        T[TMP + perm[0, j]] = one
    for _ in range(2):
        x = jnp.int32(0)
        for b in range(12, -1, -1):
            x = pick(T[TMP + b] == 0, b, x)
        T[TMP + x] = one
    for s in range(10):
        T[OCC + s] = jnp.int32(3 + s)
    for i in range(3):
        best = jnp.int32(-1)
        for s in range(10):
            good = jnp.logical_and(T[TMP + 3 + s] == 1, T[USED + s] == 0)
            best = pick(good, s, best)
        slot = jnp.where(T[TMP + i] == 1, -1, best)
        active = slot >= 0
        safe = jnp.maximum(slot, 0)
        T[USED + safe] = jnp.where(active, one, T[USED + safe])
        T[OCCL + i] = jnp.where(active, slot + 3, jnp.int32(i))
        T[OCC + safe] = jnp.where(active, jnp.int32(i), T[OCC + safe])
        T[S0 + i] = slot
        T[S0 + 20 + i] = pick(active, 1 << i, 0)
    fill_slots(T, S0, 3)
    kept = jnp.int32(0)
    sent = jnp.int32(0)
    for s in range(10):
        occ = T[OCC + s]
        is_kept = T[TMP + occ] == 1
        T[USED + s] = jnp.where(is_kept, kept, sent + 3)
        T[jnp.where(is_kept, OCCL + 3 + kept, OCCT + sent)] = occ
        kept = jnp.where(is_kept, kept + 1, kept)
        sent = jnp.where(is_kept, sent, sent + 1)
    T[OCCL + 6] = jnp.int32(RI)
    set_strides(T, S0, USED)


def make_plan_1(T):
    one = jnp.int32(1)
    u = tuple(T[U + j] for j in range(4))
    for k in range(2):
        base = G + 20 * k
        lanes = [lane_of(T, OCCL, x) for x in (RI, u[2 * k], u[2 * k + 1])]
        other_lanes(T, base, lanes)
        for p in range(3):
            T[base + p] = lanes[p]
        T[base + 3] = jnp.int32(7)
        T[base + 4] = jnp.int32(8)
    for b in range(16):
        T[TMP + b] = jnp.int32(0)
        T[USED + b] = jnp.int32(0)
    for j in range(4):
        T[TMP + u[j]] = one
    for s in range(10):
        T[OCC + s] = jnp.int32(3 + s)
    for i in range(3):
        mine_u = T[TMP + i]
        mine_ok = jnp.logical_and(mine_u == 0, T[WINV + i] < 6)
        best = jnp.int32(-1)
        spare = jnp.int32(-1)
        for b in range(3, 13):
            free = jnp.logical_and(T[TMP + b] == 0, T[USED + b - 3] == 0)
            spare = pick(free, b, spare)
            best = pick(jnp.logical_and(free, T[WINV + b] < 6), b, best)
        other = jnp.where(mine_u == 0, -1, spare)
        bit = jnp.where(mine_ok, -1, jnp.where(best >= 0, best, other))
        active = bit >= 0
        safe = jnp.maximum(bit, 3)
        T[USED + safe - 3] = jnp.where(active, one, T[USED + safe - 3])
        T[P1 + i] = jnp.where(active, bit - 3, -1)
        T[OCCR + i] = jnp.where(active, bit, jnp.int32(i))
        T[OCC + safe - 3] = jnp.where(active, jnp.int32(i), T[OCC + safe - 3])
        T[P1 + 20 + i] = pick(active, 1 << i, 0)
    fill_slots(T, P1, 3)
    rare = jnp.int32(0)
    rare_amt = jnp.int32(0)
    rare_q = jnp.int32(6)
    for i in range(3):
        q = T[WINV + T[OCCR + i]]
        bad = q >= 6
        rare = pick(bad, 1, rare)
        rare_amt = pick(bad, 1 << i, rare_amt)
        rare_q = jnp.where(bad, q, rare_q)
    other = jnp.int32(0)
    kept = jnp.int32(0)
    rare_bit = jnp.int32(0)
    for s in range(10):
        occ = T[OCC + s]
        in_u = jnp.int32(-1)
        for j in range(4):
            in_u = pick(occ == u[j], 6 + j, in_u)
        place = jnp.where(in_u >= 0, in_u, other)
        other = jnp.where(in_u >= 0, other, other + 1)
        T[TMP + s] = place
        q = T[WINV + occ]
        is_kept = q < 6
        fits = kept < 3
        bit = jnp.where(is_kept, jnp.where(fits, kept, rare_q - 3), q - 3)
        slot = jnp.where(jnp.logical_and(is_kept, fits), kept, 3)
        T[OCCR + 3 + slot] = jnp.where(is_kept, occ, jnp.int32(RI))
        rare_bit = jnp.where(jnp.logical_and(is_kept, jnp.logical_not(fits)), occ, rare_bit)
        kept = jnp.where(is_kept, kept + 1, kept)
        T[SC + place] = jnp.left_shift(one, bit)
    for i in range(3):
        q = T[WINV + T[OCCR + i]]
        T[OCCR + i] = jnp.where(q >= 6, rare_bit, T[OCCR + i])
    T[OCCR + 6] = jnp.int32(RI)
    T[RARE] = rare
    T[RARE + 1] = jnp.left_shift(one, rare_q - 3)
    T[RARE + 2] = rare_amt
    set_strides(T, P1, TMP)


def make_plan_2(T):
    one = jnp.int32(1)
    w = tuple(T[W + q] for q in range(13))
    for k in range(3):
        T[SUBC + k] = T[OCCL + k]
        T[OCC + k] = T[OCCL + 3 + k]
    for k in range(7):
        T[OCC + 3 + k] = T[OCCT + k]
    for s in range(16):
        T[USED + s] = jnp.int32(0)
    for i in range(3):
        mine = T[SUBC + i]
        best = jnp.int32(-1)
        for s in range(10):
            good = jnp.logical_and(T[WINV + T[OCC + s]] >= 4, T[USED + s] == 0)
            best = pick(good, s, best)
        slot = jnp.where(T[WINV + mine] >= 4, -1, best)
        active = slot >= 0
        safe = jnp.maximum(slot, 0)
        T[USED + safe] = jnp.where(active, one, T[USED + safe])
        new = T[OCC + safe]
        T[SUBC + i] = jnp.where(active, new, mine)
        T[OCC + safe] = jnp.where(active, mine, new)
        T[A2 + i] = slot
        T[A2 + 20 + i] = pick(active, 1 << i, 0)
    fill_slots(T, A2, 3)
    other = jnp.int32(0)
    for s in range(10):
        q = T[WINV + T[OCC + s]]
        T[TMP + s] = jnp.where(q < 4, q + 6, other)
        other = jnp.where(q < 4, other, other + 1)
    set_strides(T, A2, TMP)
    for s in range(10):
        T[USED + T[TMP + s]] = T[OCC + s]
    for s in range(10):
        T[OCC + s] = T[USED + s]
    rows = [lane_of(T, OCCR, w[q]) for q in range(6)]
    ri = lane_of(T, OCCR, RI)
    other_lanes(T, G + 40, (ri, rows[0], rows[1]))
    for k, v in enumerate((ri, 7, 8, rows[0], rows[1])):
        T[G + 40 + k] = jnp.int32(v)
    for k, v in enumerate((ri, 7, 8, rows[2], rows[3], rows[0], rows[1], rows[4], rows[5])):
        T[G + 60 + k] = jnp.int32(v)
    for k, v in enumerate((6, 7, 8, 2, 3, 0, 1, 4, 5)):
        T[G + 69 + k] = jnp.int32(v)
    for i in range(3):
        T[OCC + 6 + i] = T[SUBC + i]
    for s in range(10):
        T[USED + s] = jnp.int32(0)
        q = T[WINV + T[OCC + s]]
        T[TMP + s] = q - 7
    for k in range(4):
        slot = jnp.int32(0)
        for s in range(10):
            slot = pick(T[OCC + s] == w[3 + k], s, slot)
        T[USED + slot] = one
        T[C2 + k] = slot
        T[TMP + slot] = jnp.int32(6 + k)
    fill_slots(T, C2, 4)
    set_strides(T, C2, TMP)


def sums(start, strides):
    out = [start]
    for stride in strides:
        out = out + [o + stride for o in out]
    return out


def block_loop(src, dst, load, store, work):
    src_low = sums(jnp.int32(0), src[:3])
    dst_low = sums(jnp.int32(0), dst[:3])

    def block(b, carry):
        src_base = jnp.int32(0)
        dst_base = jnp.int32(0)
        for k in range(5):
            bit = jnp.bitwise_and(jnp.right_shift(b, k), 1)
            src_base = src_base + bit * src[5 + k]
            dst_base = dst_base + bit * dst[5 + k]
        vs = []
        for high in sums(src_base, src[3:5]):
            vs.extend(load[tile_rows(high + low), :] for low in src_low)
        vs = work(vs)
        m = 0
        for high in sums(dst_base, dst[3:5]):
            for low in dst_low:
                store[tile_rows(high + low), :] = vs[m]
                m += 1
        return carry

    lax.fori_loop(0, 32, block, 0)


def table_strides(T, base):
    return [T[base + k] * 8 for k in range(10)], [T[base + 10 + k] * 8 for k in range(10)]


def sublane_swaps(src, dst, load, store, amounts):
    sub = lax.broadcasted_iota(jnp.int32, (8, 128), 0)
    hits = [jnp.bitwise_and(sub, amount) for amount in amounts]
    keep_x = [hit == 0 for hit in hits]
    keep_y = [hit == amount for hit, amount in zip(hits, amounts)]

    def work(vs):
        for k in range(3):
            for m in range(32):
                if not m >> k & 1:
                    n = m | 1 << k
                    x, y = vs[m], vs[n]
                    vs[m] = jnp.where(keep_x[k], x, pltpu.roll(y, 1 << k, 0))
                    vs[n] = jnp.where(keep_y[k], y, pltpu.roll(x, 8 - (1 << k), 0))
        return vs

    block_loop(src, dst, load, store, work)


def table_swaps(T, base, load, store):
    src, dst = table_strides(T, base)
    sublane_swaps(src, dst, load, store, [T[base + 20 + k] for k in range(3)])


def transposes(T, base, load, store):
    src, dst = table_strides(T, base)

    def work(vs):
        out = []
        for half in range(2):
            y = jnp.concatenate(vs[16 * half : 16 * half + 16], axis=0).T
            out.extend(y[8 * m : 8 * m + 8, :] for m in range(16))
        return out

    block_loop(src, dst, load, store, work)


def turn(src, dst):
    low = lax.broadcasted_iota(jnp.int32, (64, 128), 1) < 64

    def body(d, carry):
        rows = [pl.ds(pl.multiple_of((d + k) * 64, 64), 64) for k in (0, 64)]
        y = jnp.concatenate([src[r, :] for r in rows], axis=0).T
        p, q = y[:64, :], y[64:, :]
        moved = pltpu.roll(jnp.where(low, q, p), 64, 1)
        dst[rows[0], :] = jnp.where(low, p, moved)
        dst[rows[1], :] = jnp.where(low, moved, q)
        return carry

    lax.fori_loop(0, 64, body, 0, unroll=4)


def tile_rows(row):
    return pl.ds(pl.multiple_of(row, 8), 8)


def build_matrix(T, base, out_base, sup, gh_ref, gl_ref):
    real, imag = sup[0], sup[1]
    top = jnp.concatenate([real, -imag], axis=1)
    bottom = jnp.concatenate([imag, real], axis=1)
    kern = jnp.concatenate([top, bottom], axis=0)
    index_i = lax.broadcasted_iota(jnp.int32, (512, 32), 0)
    index_o = lax.broadcasted_iota(jnp.int32, (32, 512), 1)

    def code(index, start, first, count):
        total = jnp.zeros_like(index)
        place = {0: 4, 1: 0, 2: 1, 3: 2, 4: 3}
        for k in range(first, first + count):
            bit = jnp.bitwise_and(jnp.right_shift(index, T[start + k]), 1)
            total = total + jnp.left_shift(bit, place[k] if first == 0 else k - first)
        return total

    one_i = (code(index_i, base, 0, 5) == lax.broadcasted_iota(jnp.int32, (512, 32), 1)).astype(jnp.bfloat16)
    one_o = (code(index_o, out_base, 0, 5) == lax.broadcasted_iota(jnp.int32, (32, 512), 0)).astype(jnp.bfloat16)
    rest_i = code(lax.broadcasted_iota(jnp.int32, (512, 128), 0), base, 5, 4)
    rest_o = code(lax.broadcasted_iota(jnp.int32, (8, 512), 1), out_base, 5, 4)
    same = jnp.concatenate([rest_i] * 4, axis=1) == jnp.concatenate([rest_o] * 64, axis=0)
    kh = kern.astype(jnp.bfloat16)
    kl = (kern - kh.astype(jnp.float32)).astype(jnp.bfloat16)
    for part, ref in ((kh, gh_ref), (kl, gl_ref)):
        left = lax.dot_general(one_i, part, (((1,), (1,)), ((), ())), preferred_element_type=jnp.float32)
        full = jnp.dot(left.astype(jnp.bfloat16), one_o, preferred_element_type=jnp.float32)
        ref[...] = jnp.where(same, full, 0.0).astype(jnp.bfloat16)


def mix(parts, gh, gl):
    x = jnp.concatenate(parts, axis=1)
    xh = x.astype(jnp.bfloat16)
    xl = (x - xh.astype(jnp.float32)).astype(jnp.bfloat16)
    y = jnp.dot(xl, gh, preferred_element_type=jnp.float32)
    y = y + jnp.dot(xh, gl, preferred_element_type=jnp.float32)
    return y + jnp.dot(xh, gh, preferred_element_type=jnp.float32)


def split_kernel(perm, rho, out, T, buf):
    step = pl.program_id(0)

    @pl.when(step == 0)
    def _():
        make_plan_0(perm, T)

    for c in range(8):
        lanes = slice(c * 128, c * 128 + 128)
        x = jnp.concatenate([rho[0, :, lanes], rho[1, :, lanes]], axis=0)
        buf[pl.ds(pl.multiple_of(step * 1024 + c * 128, 128), 128), :] = x.T

    @pl.when(step == 7)
    def _():
        table_swaps(T, S0, buf, out)


def prepare_kernel(first_table, sup, T, matrices):
    def copy(k, carry):
        T[k] = first_table[k]
        return carry

    lax.fori_loop(0, TMP, copy, 0)
    make_plan_1(T)
    make_plan_2(T)
    for k, (base, out_base) in enumerate(((G, G), (G + 20, G + 20), (G + 40, G + 40), (G + 60, G + 69))):
        build_matrix(T, base, out_base, sup[k // 2], matrices.at[2 * k], matrices.at[2 * k + 1])


def mix_pass(src, dst, matrices, step, store=None):
    def body(g, carry):
        first = g * 4 if step == 1 else g
        rows = [pl.ds(pl.multiple_of((first + step * j) * 512, 512), 512) for j in range(4)]
        y = mix([src[r, :] for r in rows], matrices[0], matrices[1])
        for j in range(4):
            piece = y[:, j * 128 : (j + 1) * 128]
            if store is None:
                dst[rows[j], :] = piece
            else:
                store(g, j, piece)
        return carry

    lax.fori_loop(0, 4, body, 0)


def first_kernel(T, matrices_hbm, x, out, buf, buf2, matrices, sem):
    fetch = pltpu.make_async_copy(matrices_hbm.at[pl.ds(0, 4)], matrices, sem)
    fetch.start()
    turn(x, buf)
    table_swaps(T, P1, buf, buf2)
    fetch.wait()
    mix_pass(buf2, buf2, matrices.at[pl.ds(0, 2)], 1)
    strides = [T[SC + k] * 8 for k in range(10)]
    low = [jnp.int32(0)]
    for k in range(3):
        low = low + [o + strides[k] for o in low]

    def scatter(h, j, piece):
        start = jnp.bitwise_and(h, 1) * strides[6] + jnp.right_shift(h, 1) * strides[7]
        if j & 1:
            start = start + strides[8]
        if j & 2:
            start = start + strides[9]
        high = [start]
        for k in range(3, 6):
            high = high + [o + strides[k] for o in high]
        for n in range(64):
            out[tile_rows(high[n >> 3] + low[n & 7]), :] = piece[n * 8 : n * 8 + 8, :]

    mix_pass(buf2, None, matrices.at[pl.ds(2, 2)], 4, scatter)

    @pl.when(T[RARE] == 1)
    def _():
        stride = T[RARE + 1]
        amount = T[RARE + 2]
        sub = lax.broadcasted_iota(jnp.int32, (8, 128), 0)
        hit = jnp.bitwise_and(sub, amount)

        def pair(b, carry):
            low = jnp.bitwise_and(b, stride - 1)
            t = (b - low) * 2 + low
            a_rows, b_rows = tile_rows(t * 8), tile_rows((t + stride) * 8)
            a, c = out[a_rows, :], out[b_rows, :]
            up = pltpu.roll(c, amount, 0)
            down = pltpu.roll(a, 8 - amount, 0)
            out[a_rows, :] = jnp.where(hit == 0, a, up)
            out[b_rows, :] = jnp.where(hit == amount, c, down)
            return carry

        lax.fori_loop(0, 512, pair, 0)


def second_kernel(T, pos, matrices_hbm, x, out, trace, buf, buf2, matrices, sem):
    fetch = pltpu.make_async_copy(matrices_hbm.at[pl.ds(4, 4)], matrices, sem)
    fetch.start()
    turn(x, buf)
    table_swaps(T, A2, buf, buf2)
    fetch.wait()
    mix_pass(buf2, buf, matrices.at[pl.ds(0, 2)], 1)
    mix_pass(buf, buf2, matrices.at[pl.ds(2, 2)], 4)
    slots = [8 << k for k in (6, 7, 8, 0, 1, 2, 3, 4, 5, 9)]
    sublane_swaps(slots, slots, buf2, buf, (1, 2, 4))
    transposes(T, C2, buf, out)
    device = pos[0]
    column = jnp.right_shift(device, 1)
    shift = jnp.bitwise_and(device, 1) * 64
    sub = lax.broadcasted_iota(jnp.int32, (8, 128), 0)
    lane = lax.broadcasted_iota(jnp.int32, (8, 128), 1)
    total = jnp.zeros((8, 128), jnp.float32)
    for t in range(8):
        tile = out[tile_rows((t * 64 + column) * 8), :]
        total = total + jnp.where(lane == sub + (t * 8 + shift), tile, 0.0)
    trace[0, 0] = jnp.sum(total)


SMEM = pl.BlockSpec(memory_space=pltpu.SMEM)
VMEM = pl.BlockSpec(memory_space=pltpu.VMEM)
HBM = pl.BlockSpec(memory_space=pl.ANY)
LIMIT = 60 << 20
BUFFER = pltpu.VMEM((8192, 128), jnp.float32)
MATRICES = pltpu.VMEM((4, 512, 512), jnp.bfloat16)


def exchange(blocks):
    return lax.all_to_all(blocks, AX, split_axis=0, concat_axis=0, tiled=True)


def per_device(rho, perm, superop):
    blocks, table = pl.pallas_call(
        split_kernel,
        grid=(8,),
        in_specs=[SMEM, pl.BlockSpec((2, 64, 1024), lambda i: (0, 0, i))],
        out_specs=[pl.BlockSpec((8192, 128), lambda i: (0, 0)), SMEM],
        scratch_shapes=[BUFFER],
        out_shape=[
            jax.ShapeDtypeStruct((8192, 128), jnp.float32),
            jax.ShapeDtypeStruct((SIZE,), jnp.int32),
        ],
        compiler_params=pltpu.CompilerParams(vmem_limit_bytes=LIMIT),
        name="split",
    )(perm, rho)
    table, matrices = pl.pallas_call(
        prepare_kernel,
        in_specs=[SMEM, VMEM],
        out_specs=[SMEM, VMEM],
        out_shape=[
            jax.ShapeDtypeStruct((SIZE,), jnp.int32),
            jax.ShapeDtypeStruct((8, 512, 512), jnp.bfloat16),
        ],
        compiler_params=pltpu.CompilerParams(vmem_limit_bytes=LIMIT),
        name="prepare",
    )(table, superop)
    blocks = exchange(blocks.reshape(128, 64, 128))
    blocks = pl.pallas_call(
        first_kernel,
        in_specs=[SMEM, HBM, VMEM],
        out_specs=VMEM,
        out_shape=jax.ShapeDtypeStruct((8192, 128), jnp.float32),
        scratch_shapes=[BUFFER, BUFFER, MATRICES, pltpu.SemaphoreType.DMA],
        compiler_params=pltpu.CompilerParams(vmem_limit_bytes=LIMIT),
        name="first",
    )(table, matrices, blocks.reshape(8192, 128))
    blocks = exchange(blocks.reshape(128, 64, 128))
    device = lax.axis_index(AX).astype(jnp.int32).reshape(1)
    tiles, trace = pl.pallas_call(
        second_kernel,
        in_specs=[SMEM, SMEM, HBM, VMEM],
        out_specs=[VMEM, SMEM],
        out_shape=[
            jax.ShapeDtypeStruct((8192, 128), jnp.float32),
            jax.ShapeDtypeStruct((1, 1), jnp.float32),
        ],
        scratch_shapes=[BUFFER, BUFFER, MATRICES, pltpu.SemaphoreType.DMA],
        compiler_params=pltpu.CompilerParams(vmem_limit_bytes=LIMIT),
        name="second",
    )(table, device, matrices, blocks.reshape(8192, 128))
    rho_out = tiles.reshape(2, 8, 64, 8, 128).transpose(0, 1, 3, 2, 4).reshape(2, 64, 8192)
    parts = exchange(jnp.broadcast_to(trace[0, 0], (128, 1, 128)))
    return rho_out, jnp.sum(parts[:, 0, 0]) / ROWS


def solution(mesh):
    spec = P(None, AX, None)
    return jax.shard_map(
        per_device, mesh=mesh, in_specs=(spec, P(), P()), out_specs=(spec, P()), check_vma=False
    )
```

time: 208 us -> 195 us (0.938)
  Pallas kernels: 72.3 us -> 59 us
    pallas_call x1, Pallas kernels: 33.4 us -> 22.3 us  [per_device(): pl.pallas_call(second_kernel, in_specs=[SMEM, SMEM, HBM, VMEM], out_specs...]
    pallas_call x1, Pallas kernels: 15.4 us -> 9.85 us  [per_device(): pl.pallas_call(split_kernel, grid=(8,), in_specs=[SMEM, pl.BlockSpec((2,...]
    pallas_call x1, Pallas kernels: 14.4 us -> 17.8 us  [per_device(): pl.pallas_call(first_kernel, in_specs=[SMEM, HBM, VMEM], out_specs=VMEM,...]
  transfers between devices with their start and end apart: 2 -> 2, of which waited for: 2 -> 2; matrix products, arithmetic and copies ran while one was open for 0% -> 0% of each run, Pallas kernels for 4% -> 5%
where the time goes in v3:
time: 195 us; the launch traced here: 194 us
  waiting for transfers between devices  98.9 us (51%)
  Pallas kernels  59 us (30%)
  starting transfers between devices  17.8 us (9%)
  blocking collectives  14.8 us (8%)
  between operations  2.47 us (1%)
    all_to_all x2, waiting for transfers between devices, exchange(): return lax.all_to_all(blocks, AX, split_axis=0, concat_axis=0, tiled=True)  98.9 us
    pallas_call x1, Pallas kernels, per_device(): pl.pallas_call(second_kernel, in_specs=[SMEM, SMEM, HBM, VMEM], out_specs...  22.3 us
    all_to_all x2, starting transfers between devices, exchange(): return lax.all_to_all(blocks, AX, split_axis=0, concat_axis=0, tiled=True)  17.8 us
    pallas_call x1, Pallas kernels, per_device(): pl.pallas_call(first_kernel, in_specs=[SMEM, HBM, VMEM], out_specs=VMEM,...  17.8 us
    all_to_all x1, blocking collectives, exchange(): return lax.all_to_all(blocks, AX, split_axis=0, concat_axis=0, tiled=True)  14.8 us
    pallas_call x1, Pallas kernels, per_device(): pl.pallas_call(split_kernel, grid=(8,), in_specs=[SMEM, pl.BlockSpec((2,...  9.85 us
    pallas_call x1, Pallas kernels, per_device(): pl.pallas_call(prepare_kernel, in_specs=[SMEM, VMEM], out_specs=[SMEM, VM...  9.08 us
  transfers between devices with their start and end apart: 2, of which 2 were waited for; matrix products, arithmetic and copies ran while one was open for 0% of the time, Pallas kernels for 5%

profile of v3, /device:TPU:1, one launch (start us, length us, event | category | flops | bytes accessed | tf_op | source)
XLA Modules:
  0.0 194.4 jit_solution(15794984832803117204)
XLA Ops:
  0.6 9.9 %split.1 = (f32[8192,128]{1,0:T(8,128)}, s32[432]{0:T(512)}) custom-call(s32[2,13]{1,0:T(2,128)} %perm.1, f32[2,64,8192]{2,1,0:T(8,128)} %rho.1), custom_call_target="tpu_custom_call" | custom-call | tf_op jit(solution)/shard_map/split/pallas_call | solution.py:518
  10.5 12.0 %all-to-all-start = ((f32[128,64,128]{2,1,0:T(8,128)}), f32[128,64,128]{2,1,0:T(8,128)}, u32[]{:S(2)}, u32[]{:S(2)}) async-start(f32[128,64,128]{2,1,0:T(8,128)} %bitcast.12), calls=%async_computation | async-start | bytes 8388608 | tf_op jit(solution)/shard_map/all_to_all | solution.py:514
  22.4 9.1 %prepare.1 = (s32[432]{0:T(512)}, bf16[8,512,512]{2,1,0:T(8,128)(2,1)}) custom-call(s32[432]{0:T(512)} %get-tuple-element.8.first_table, f32[2,2,16,16]{3,2,1,0:T(8,128)} %sup.1), custom_call_target="tpu_custom_call" | custom-call | tf_op jit(solution)/shard_map/prepare/pallas_call | solution.py:531
  31.5 44.9 %all-to-all-done = f32[128,64,128]{2,1,0:T(8,128)} async-done(((f32[128,64,128]{2,1,0:T(8,128)}), f32[128,64,128]{2,1,0:T(8,128)}, u32[]{:S(2)}, u32[]{:S(2)}) %all-to-all-start) | async-done | bytes 4194336 | tf_op jit(solution)/shard_map/all_to_all | solution.py:514
  76.5 17.8 %first.1 = f32[8192,128]{1,0:T(8,128)} custom-call(s32[432]{0:T(512)} %get-tuple-element.9.T, bf16[8,512,512]{2,1,0:T(8,128)(2,1)} %get-tuple-element.10.matrices_hbm, f32[8192,128]{1,0:T(8,128)} %bitcast.2.x), custom_call_target="tpu_custom_call" | custom-call | tf_op jit(solution)/shard_map/first/pallas_call | solution.py:543
  94.3 5.9 %all-to-all-start.1 = ((f32[128,64,128]{2,1,0:T(8,128)}), f32[128,64,128]{2,1,0:T(8,128)}, u32[]{:S(2)}, u32[]{:S(2)}) async-start(f32[128,64,128]{2,1,0:T(8,128)} %bitcast.11), calls=%async_computation.1 | async-start | bytes 8388608 | tf_op jit(solution)/shard_map/all_to_all | solution.py:514
  100.1 54.0 %all-to-all-done.1 = f32[128,64,128]{2,1,0:T(8,128)} async-done(((f32[128,64,128]{2,1,0:T(8,128)}), f32[128,64,128]{2,1,0:T(8,128)}, u32[]{:S(2)}, u32[]{:S(2)}) %all-to-all-start.1) | async-done | bytes 4194336 | tf_op jit(solution)/shard_map/all_to_all | solution.py:514
  154.1 22.3 %second.1 = (f32[8192,128]{1,0:T(8,128)}, f32[1,1]{1,0:T(1,128)}) custom-call(s32[432]{0:T(512)} %get-tuple-element.9.T, s32[1]{0:T(128)} %bitcast.pos, bf16[8,512,512]{2,1,0:T(8,128)(2,1)} %get-tuple-element.10.matrices_hbm, f32[8192,128]{1,0:T(8,128)} %bitcast.4.x), custom_call_target="tpu_custom_call" | custom-call | tf_op jit(solution)/shard_map/second/pallas_call | solution.py:554
  176.4 0.7 broadcast_in_dim.3
  177.1 14.8 %all_to_all.15 = f32[128,1,128]{2,1,0:T(1,128)S(1)} all-to-all(f32[128,1,128]{2,1,0:T(1,128)S(1)} %broadcast_in_dim.3), channel_id=1, replica_groups=mesh['hi'=64,'grp'=2] {'hi','grp'}, dimensions={0} | all-to-all | bytes 131072 | tf_op jit(solution)/shard_map/all_to_all | solution.py:514
  191.9 0.7 slice_reduce_fusion
Async XLA Ops:
  10.5 66.0 %all-to-all-start = ((f32[128,64,128]{2,1,0:T(8,128)}), f32[128,64,128]{2,1,0:T(8,128)}, u32[]{:S(2)}, u32[]{:S(2)}) async-start(f32[128,64,128]{2,1,0:T(8,128)} %bitcast.12), calls=%async_computation | async-start | bytes 8388608 | tf_op jit(solution)/shard_map/all_to_all | solution.py:514
  94.3 59.9 %all-to-all-start.1 = ((f32[128,64,128]{2,1,0:T(8,128)}), f32[128,64,128]{2,1,0:T(8,128)}, u32[]{:S(2)}, u32[]{:S(2)}) async-start(f32[128,64,128]{2,1,0:T(8,128)} %bitcast.11), calls=%async_computation.1 | async-start | bytes 8388608 | tf_op jit(solution)/shard_map/all_to_all | solution.py:514

commit v4 on v3

--- a/solution.py
+++ b/solution.py
@@ -243,17 +243,14 @@
     for i in range(3):
         T[OCC + 6 + i] = T[SUBC + i]
     for s in range(10):
-        T[USED + s] = jnp.int32(0)
-        q = T[WINV + T[OCC + s]]
-        T[TMP + s] = q - 7
-    for k in range(4):
+        T[TMP + s] = T[WINV + T[OCC + s]] - 7
+    for k in range(10):
         slot = jnp.int32(0)
         for s in range(10):
             slot = pick(T[OCC + s] == w[3 + k], s, slot)
-        T[USED + slot] = one
         T[C2 + k] = slot
-        T[TMP + slot] = jnp.int32(6 + k)
-    fill_slots(T, C2, 4)
+        if k < 4:
+            T[TMP + slot] = jnp.int32(6 + k)
     set_strides(T, C2, TMP)
 
 
@@ -264,7 +261,7 @@
     return out
 
 
-def block_loop(src, dst, load, store, work):
+def block_loop(src, dst, load, store, work, first=0, last=32):
     src_low = sums(jnp.int32(0), src[:3])
     dst_low = sums(jnp.int32(0), dst[:3])
 
@@ -286,7 +283,7 @@
                 m += 1
         return carry
 
-    lax.fori_loop(0, 32, block, 0)
+    lax.fori_loop(first, last, block, 0)
 
 
 def table_strides(T, base):
@@ -317,7 +314,7 @@
     sublane_swaps(src, dst, load, store, [T[base + 20 + k] for k in range(3)])
 
 
-def transposes(T, base, load, store):
+def transposes(T, base, load, store, first, last):
     src, dst = table_strides(T, base)
 
     def work(vs):
@@ -327,22 +324,36 @@
             out.extend(y[8 * m : 8 * m + 8, :] for m in range(16))
         return out
 
-    block_loop(src, dst, load, store, work)
-
-
-def turn(src, dst):
+    block_loop(src, dst, load, store, work, first, last)
+
+
+def turn(hbm, src, dst, sems):
     low = lax.broadcasted_iota(jnp.int32, (64, 128), 1) < 64
 
-    def body(d, carry):
-        rows = [pl.ds(pl.multiple_of((d + k) * 64, 64), 64) for k in (0, 64)]
-        y = jnp.concatenate([src[r, :] for r in rows], axis=0).T
-        p, q = y[:64, :], y[64:, :]
-        moved = pltpu.roll(jnp.where(low, q, p), 64, 1)
-        dst[rows[0], :] = jnp.where(low, p, moved)
-        dst[rows[1], :] = jnp.where(low, moved, q)
+    def copies(c):
+        out = []
+        for half in range(2):
+            rows = pl.ds(pl.multiple_of(half * 4096 + c * 256, 256), 256)
+            out.append(pltpu.make_async_copy(hbm.at[rows], src.at[rows], sems.at[half, c]))
+        return out
+
+    for c in range(16):
+        for copy in copies(c):
+            copy.start()
+
+    def body(c, carry):
+        for copy in copies(c):
+            copy.wait()
+        for k in range(4):
+            rows = [pl.ds(pl.multiple_of(half * 4096 + c * 256 + k * 64, 64), 64) for half in range(2)]
+            y = jnp.concatenate([src[r, :] for r in rows], axis=0).T
+            p, q = y[:64, :], y[64:, :]
+            moved = pltpu.roll(jnp.where(low, q, p), 64, 1)
+            dst[rows[0], :] = jnp.where(low, p, moved)
+            dst[rows[1], :] = jnp.where(low, moved, q)
         return carry
 
-    lax.fori_loop(0, 64, body, 0, unroll=4)
+    lax.fori_loop(0, 16, body, 0)
 
 
 def tile_rows(row):
@@ -432,10 +443,10 @@
     lax.fori_loop(0, 4, body, 0)
 
 
-def first_kernel(T, matrices_hbm, x, out, buf, buf2, matrices, sem):
+def first_kernel(T, matrices_hbm, x, out, buf, buf2, matrices, sem, sems):
     fetch = pltpu.make_async_copy(matrices_hbm.at[pl.ds(0, 4)], matrices, sem)
     fetch.start()
-    turn(x, buf)
+    turn(x, buf2, buf, sems)
     table_swaps(T, P1, buf, buf2)
     fetch.wait()
     mix_pass(buf2, buf2, matrices.at[pl.ds(0, 2)], 1)
@@ -479,27 +490,86 @@
         lax.fori_loop(0, 512, pair, 0)
 
 
-def second_kernel(T, pos, matrices_hbm, x, out, trace, buf, buf2, matrices, sem):
+def second_kernel(T, matrices_hbm, x, out, buf, buf2, matrices, sem, sems):
     fetch = pltpu.make_async_copy(matrices_hbm.at[pl.ds(4, 4)], matrices, sem)
     fetch.start()
-    turn(x, buf)
+    turn(x, buf2, buf, sems)
     table_swaps(T, A2, buf, buf2)
     fetch.wait()
     mix_pass(buf2, buf, matrices.at[pl.ds(0, 2)], 1)
     mix_pass(buf, buf2, matrices.at[pl.ds(2, 2)], 4)
     slots = [8 << k for k in (6, 7, 8, 0, 1, 2, 3, 4, 5, 9)]
     sublane_swaps(slots, slots, buf2, buf, (1, 2, 4))
-    transposes(T, C2, buf, out)
-    device = pos[0]
-    column = jnp.right_shift(device, 1)
-    shift = jnp.bitwise_and(device, 1) * 64
+    tiles = buf2.reshape(16, 512, 128)
+    sends = []
+    for c in range(4):
+        transposes(T, C2, buf, buf2, 8 * c, 8 * c + 8)
+        part = pl.ds(c * 128, 128)
+        sends.append(pltpu.make_async_copy(tiles.at[:, part], out.at[:, part], sems.at[0, c]))
+        sends[-1].start()
+    for send in sends:
+        send.wait()
+
+
+def trace_kernel(T, pos, sup, x, out):
+    step = pl.program_id(0)
+    lane = lax.broadcasted_iota(jnp.int32, (8, 128), 1)
     sub = lax.broadcasted_iota(jnp.int32, (8, 128), 0)
-    lane = lax.broadcasted_iota(jnp.int32, (8, 128), 1)
-    total = jnp.zeros((8, 128), jnp.float32)
-    for t in range(8):
-        tile = out[tile_rows((t * 64 + column) * 8), :]
-        total = total + jnp.where(lane == sub + (t * 8 + shift), tile, 0.0)
-    trace[0, 0] = jnp.sum(total)
+
+    def bit_at(index, k, place):
+        return jnp.left_shift(jnp.bitwise_and(jnp.right_shift(index, k), 1), place)
+
+    col_base = jnp.int32(0)
+    for k in range(7):
+        col_base = col_base + bit_at(pos[0], k, T[WINV + T[OCCT + k]])
+    col = jnp.zeros_like(lane) + col_base
+    for k in range(6):
+        col = col + bit_at(lane, k, T[WINV + T[OCCL + k]])
+    row_sub = jnp.zeros_like(sub)
+    for k in range(3):
+        row_sub = row_sub + bit_at(sub, k, T[WINV + T[OCCR + k]])
+    row_places = [T[WINV + T[OCCR + 3 + k]] for k in range(3)]
+    tables = []
+    for pair in range(2):
+        v = jnp.bitwise_and(jnp.right_shift(col, 2 * pair), 3)
+        for part in range(2):
+            for a in range(4):
+                value = jnp.zeros((8, 128), jnp.float32)
+                for b in range(4):
+                    index = 4 * a + b
+                    total = sup[part, 0, index] + sup[part, 5, index]
+                    total = total + sup[part, 10, index] + sup[part, 15, index]
+                    value = jnp.where(v == b, total, value)
+                tables.append(value)
+    imag = lane >= 64
+    high = jnp.right_shift(col, 4)
+
+    def tile(n, total):
+        g = step * 64 + n
+        row = jnp.right_shift(g, 3) * 64
+        for k in range(3):
+            row = row + bit_at(g, k, row_places[k])
+        row = row_sub + row
+        factors = []
+        for pair in range(2):
+            u = jnp.bitwise_and(jnp.right_shift(row, 2 * pair), 3)
+            for part in range(2):
+                value = tables[8 * pair + 4 * part]
+                for a in range(1, 4):
+                    value = jnp.where(u == a, tables[8 * pair + 4 * part + a], value)
+                factors.append(value)
+        r0, i0, r1, i1 = factors
+        weight = jnp.where(imag, -(r0 * i1 + i0 * r1), r0 * r1 - i0 * i1)
+        data = x[tile_rows(n * 8), :]
+        return total + jnp.where(jnp.right_shift(row, 4) == high, weight * data, 0.0)
+
+    total = lax.fori_loop(0, 64, tile, jnp.zeros((8, 128), jnp.float32), unroll=4)
+
+    @pl.when(step == 0)
+    def _():
+        out[0, 0] = jnp.float32(0.0)
+
+    out[0, 0] = out[0, 0] + jnp.sum(total)
 
 
 SMEM = pl.BlockSpec(memory_space=pltpu.SMEM)
@@ -508,6 +578,7 @@
 LIMIT = 60 << 20
 BUFFER = pltpu.VMEM((8192, 128), jnp.float32)
 MATRICES = pltpu.VMEM((4, 512, 512), jnp.bfloat16)
+SCRATCH = [BUFFER, BUFFER, MATRICES, pltpu.SemaphoreType.DMA, pltpu.SemaphoreType.DMA((2, 16))]
 
 
 def exchange(blocks):
@@ -542,29 +613,35 @@
     blocks = exchange(blocks.reshape(128, 64, 128))
     blocks = pl.pallas_call(
         first_kernel,
-        in_specs=[SMEM, HBM, VMEM],
+        in_specs=[SMEM, HBM, HBM],
         out_specs=VMEM,
         out_shape=jax.ShapeDtypeStruct((8192, 128), jnp.float32),
-        scratch_shapes=[BUFFER, BUFFER, MATRICES, pltpu.SemaphoreType.DMA],
+        scratch_shapes=SCRATCH,
         compiler_params=pltpu.CompilerParams(vmem_limit_bytes=LIMIT),
         name="first",
     )(table, matrices, blocks.reshape(8192, 128))
+    device = lax.axis_index(AX).astype(jnp.int32).reshape(1)
+    trace = pl.pallas_call(
+        trace_kernel,
+        grid=(16,),
+        in_specs=[SMEM, SMEM, SMEM, pl.BlockSpec((512, 128), lambda i: (i, 0))],
+        out_specs=SMEM,
+        out_shape=jax.ShapeDtypeStruct((1, 1), jnp.float32),
+        name="trace",
+    )(table, device, superop[1], blocks)
     blocks = exchange(blocks.reshape(128, 64, 128))
-    device = lax.axis_index(AX).astype(jnp.int32).reshape(1)
-    tiles, trace = pl.pallas_call(
+    blocks, trace = lax.optimization_barrier((blocks, trace))
+    parts = exchange(jnp.broadcast_to(trace[0, 0], (128, 1, 128)))
+    tiles = pl.pallas_call(
         second_kernel,
-        in_specs=[SMEM, SMEM, HBM, VMEM],
-        out_specs=[VMEM, SMEM],
-        out_shape=[
-            jax.ShapeDtypeStruct((8192, 128), jnp.float32),
-            jax.ShapeDtypeStruct((1, 1), jnp.float32),
-        ],
-        scratch_shapes=[BUFFER, BUFFER, MATRICES, pltpu.SemaphoreType.DMA],
+        in_specs=[SMEM, HBM, HBM],
+        out_specs=HBM,
+        out_shape=jax.ShapeDtypeStruct((16, 512, 128), jnp.float32),
+        scratch_shapes=SCRATCH,
         compiler_params=pltpu.CompilerParams(vmem_limit_bytes=LIMIT),
         name="second",
-    )(table, device, matrices, blocks.reshape(8192, 128))
+    )(table, matrices, blocks.reshape(8192, 128))
     rho_out = tiles.reshape(2, 8, 64, 8, 128).transpose(0, 1, 3, 2, 4).reshape(2, 64, 8192)
-    parts = exchange(jnp.broadcast_to(trace[0, 0], (128, 1, 128)))
     return rho_out, jnp.sum(parts[:, 0, 0]) / ROWS
 
 

time: 195 us -> 187 us (0.959); the launches traced: 194 us -> 189 us
  Pallas kernels: 59 us -> 77.2 us
  waiting for transfers between devices: 98.9 us -> 83.3 us
  blocking collectives: 14.8 us -> 0 us
  starting transfers between devices: 17.8 us -> 23.2 us
    pallas_call x2 -> x3, Pallas kernels: 40.1 us -> 58.4 us  [the longest x1 22.2 us: per_device(): pl.pallas_call(first_kernel, in_specs=[SMEM, HBM, HBM], out_specs=VMEM, o...]
    all_to_all x2 -> x3, waiting for transfers between devices: 98.9 us -> 83.3 us  [exchange(): return lax.all_to_all(blocks, AX, split_axis=0, concat_axis=0, tiled=True)]
    all_to_all x1 -> x0, blocking collectives: 14.8 us -> none  [exchange(): return lax.all_to_all(blocks, AX, split_axis=0, concat_axis=0, tiled=True)]
    all_to_all x2 -> x3, starting transfers between devices: 17.8 us -> 23.2 us  [exchange(): return lax.all_to_all(blocks, AX, split_axis=0, concat_axis=0, tiled=True)]
  transfers between devices with their start and end apart: 2 -> 3, of which waited for: 2 -> 2; matrix products, arithmetic and copies ran while one was open for 0% -> 0% of each run, Pallas kernels for 5% -> 24%
where the time goes in v4:
time: 187 us; the launch traced here: 189 us
  waiting for transfers between devices  83.3 us (45%)
  Pallas kernels  77.2 us (41%)
  starting transfers between devices  23.2 us (12%)
  between operations  2.5 us (1%)
    all_to_all x3, waiting for transfers between devices, exchange(): return lax.all_to_all(blocks, AX, split_axis=0, concat_axis=0, tiled=True)  83.3 us
    all_to_all x3, starting transfers between devices, exchange(): return lax.all_to_all(blocks, AX, split_axis=0, concat_axis=0, tiled=True)  23.2 us
    pallas_call x1, Pallas kernels, per_device(): pl.pallas_call(first_kernel, in_specs=[SMEM, HBM, HBM], out_specs=VMEM, o...  22.2 us
    pallas_call x1, Pallas kernels, per_device(): pl.pallas_call(second_kernel, in_specs=[SMEM, HBM, HBM], out_specs=HBM, o...  21 us
    pallas_call x1, Pallas kernels, per_device(): pl.pallas_call(trace_kernel, grid=(16,), in_specs=[SMEM, SMEM, SMEM, pl.B...  15.1 us
    pallas_call x1, Pallas kernels, per_device(): pl.pallas_call(split_kernel, grid=(8,), in_specs=[SMEM, pl.BlockSpec((2,...  9.85 us
    pallas_call x1, Pallas kernels, per_device(): pl.pallas_call(prepare_kernel, in_specs=[SMEM, VMEM], out_specs=[SMEM, VM...  8.96 us
  transfers between devices with their start and end apart: 3, of which 2 were waited for; matrix products, arithmetic and copies ran while one was open for 0% of the time, Pallas kernels for 24%

profile of v4, /device:TPU:1, one launch (start us, length us, event | category | flops | bytes accessed | tf_op | source)
XLA Modules:
  0.0 188.8 jit_solution(10115699356549065142)
XLA Ops:
  0.6 9.9 %split.1 = (f32[8192,128]{1,0:T(8,128)}, s32[432]{0:T(512)}) custom-call(s32[2,13]{1,0:T(2,128)} %perm.1, f32[2,64,8192]{2,1,0:T(8,128)} %rho.1), custom_call_target="tpu_custom_call" | custom-call | tf_op jit(solution)/shard_map/split/pallas_call | solution.py:589
  10.5 12.0 %all-to-all-start = ((f32[128,64,128]{2,1,0:T(8,128)}), f32[128,64,128]{2,1,0:T(8,128)}, u32[]{:S(2)}, u32[]{:S(2)}) async-start(f32[128,64,128]{2,1,0:T(8,128)} %bitcast.15), calls=%async_computation | async-start | bytes 8388608 | tf_op jit(solution)/shard_map/all_to_all | solution.py:585
  22.4 9.0 %prepare.1 = (s32[432]{0:T(512)}, bf16[8,512,512]{2,1,0:T(8,128)(2,1)}) custom-call(s32[432]{0:T(512)} %get-tuple-element.8.first_table, f32[2,2,16,16]{3,2,1,0:T(8,128)} %sup.1), custom_call_target="tpu_custom_call" | custom-call | tf_op jit(solution)/shard_map/prepare/pallas_call | solution.py:602
  31.4 45.0 %all-to-all-done = f32[128,64,128]{2,1,0:T(8,128)} async-done(((f32[128,64,128]{2,1,0:T(8,128)}), f32[128,64,128]{2,1,0:T(8,128)}, u32[]{:S(2)}, u32[]{:S(2)}) %all-to-all-start) | async-done | bytes 4194336 | tf_op jit(solution)/shard_map/all_to_all | solution.py:585
  76.5 22.2 %first.1.x = f32[8192,128]{1,0:T(8,128)} custom-call(s32[432]{0:T(512)} %get-tuple-element.9.T, bf16[8,512,512]{2,1,0:T(8,128)(2,1)} %get-tuple-element.10.matrices_hbm, f32[8192,128]{1,0:T(8,128)} %bitcast.1.x), custom_call_target="tpu_custom_call" | custom-call | tf_op jit(solution)/shard_map/first/pallas_call | solution.py:614
  98.7 0.0 copy-start
  98.7 5.9 %all-to-all-start.1 = ((f32[128,64,128]{2,1,0:T(8,128)}), f32[128,64,128]{2,1,0:T(8,128)}, u32[]{:S(2)}, u32[]{:S(2)}) async-start(f32[128,64,128]{2,1,0:T(8,128)} %bitcast.13), calls=%async_computation.1 | async-start | bytes 8388608 | tf_op jit(solution)/shard_map/all_to_all | solution.py:585
  104.5 0.0 copy-done
  104.6 0.6 slice_bitcast_fusion.sup
  105.2 15.1 %trace.1 = f32[1,1]{1,0:T(1,128)} custom-call(s32[432]{0:T(512)} %get-tuple-element.9.T, s32[1]{0:T(128)} %bitcast.3.pos, f32[2,16,16]{2,1,0:T(8,128)} %slice_bitcast_fusion.sup, f32[8192,128]{1,0:T(8,128)} %first.1.x), custom_call_target="tpu_custom_call" | custom-call | tf_op jit(solution)/shard_map/trace/pallas_call | solution.py:624
  120.3 38.2 %all-to-all-done.1 = f32[128,64,128]{2,1,0:T(8,128)} async-done(((f32[128,64,128]{2,1,0:T(8,128)}), f32[128,64,128]{2,1,0:T(8,128)}, u32[]{:S(2)}, u32[]{:S(2)}) %all-to-all-start.1) | async-done | bytes 4194336 | tf_op jit(solution)/shard_map/all_to_all | solution.py:585
  158.5 1.2 broadcast_in_dim.3
  159.8 5.4 %all-to-all-start.2 = ((f32[128,1,128]{2,1,0:T(1,128)}), f32[128,1,128]{2,1,0:T(1,128)S(1)}, u32[]{:S(2)}, u32[]{:S(2)}) async-start(f32[128,1,128]{2,1,0:T(1,128)} %broadcast_in_dim.3), calls=%async_computation.2 | async-start | bytes 131072 | tf_op jit(solution)/shard_map/all_to_all | solution.py:585
  165.2 21.0 %second.1 = f32[16,512,128]{2,1,0:T(8,128)} custom-call(s32[432]{0:T(512)} %get-tuple-element.9.T, bf16[8,512,512]{2,1,0:T(8,128)(2,1)} %get-tuple-element.10.matrices_hbm, f32[8192,128]{1,0:T(8,128)} %bitcast.5.x), custom_call_target="tpu_custom_call" | custom-call | tf_op jit(solution)/shard_map/second/pallas_call | solution.py:635
  186.2 0.0 all-to-all-done.2
  186.2 0.7 slice_reduce_fusion
Async XLA Ops:
  10.5 66.0 %all-to-all-start = ((f32[128,64,128]{2,1,0:T(8,128)}), f32[128,64,128]{2,1,0:T(8,128)}, u32[]{:S(2)}, u32[]{:S(2)}) async-start(f32[128,64,128]{2,1,0:T(8,128)} %bitcast.15), calls=%async_computation | async-start | bytes 8388608 | tf_op jit(solution)/shard_map/all_to_all | solution.py:585
  98.7 5.9 %copy-start = (f32[2,2,16,16]{3,2,1,0:T(8,128)S(1)}, f32[2,2,16,16]{3,2,1,0:T(8,128)}, u32[]{:S(2)}) copy-start(f32[2,2,16,16]{3,2,1,0:T(8,128)} %sup.1) | copy-start | bytes 12292
  98.7 59.9 %all-to-all-start.1 = ((f32[128,64,128]{2,1,0:T(8,128)}), f32[128,64,128]{2,1,0:T(8,128)}, u32[]{:S(2)}, u32[]{:S(2)}) async-start(f32[128,64,128]{2,1,0:T(8,128)} %bitcast.13), calls=%async_computation.1 | async-start | bytes 8388608 | tf_op jit(solution)/shard_map/all_to_all | solution.py:585
  159.8 26.5 %all-to-all-start.2 = ((f32[128,1,128]{2,1,0:T(1,128)}), f32[128,1,128]{2,1,0:T(1,128)S(1)}, u32[]{:S(2)}, u32[]{:S(2)}) async-start(f32[128,1,128]{2,1,0:T(1,128)} %broadcast_in_dim.3), calls=%async_computation.2 | async-start | bytes 131072 | tf_op jit(solution)/shard_map/all_to_all | solution.py:585

commit v5 on v4

--- a/solution.py
+++ b/solution.py
@@ -105,10 +105,22 @@
         T[OCC + safe] = jnp.where(active, jnp.int32(i), T[OCC + safe])
         T[S0 + i] = slot
         T[S0 + 20 + i] = pick(active, 1 << i, 0)
-    fill_slots(T, S0, 3)
+    for k in range(10):
+        free = jnp.int32(0)
+        best = jnp.int32(-1)
+        for s in range(10):
+            unused = T[USED + s] == 0
+            free = pick(unused, s, free)
+            best = pick(jnp.logical_and(unused, T[TMP + T[OCC + s]] == 1), s, best)
+        free = jnp.where(best >= 0, best, free)
+        if k < 3:
+            free = jnp.where(T[S0 + k] >= 0, T[S0 + k], free)
+        T[USED + free] = one
+        T[S0 + k] = free
     kept = jnp.int32(0)
     sent = jnp.int32(0)
-    for s in range(10):
+    for k in range(10):
+        s = T[S0 + k]
         occ = T[OCC + s]
         is_kept = T[TMP + occ] == 1
         T[USED + s] = jnp.where(is_kept, kept, sent + 3)
@@ -290,7 +302,7 @@
     return [T[base + k] * 8 for k in range(10)], [T[base + 10 + k] * 8 for k in range(10)]
 
 
-def sublane_swaps(src, dst, load, store, amounts):
+def sublane_swaps(src, dst, load, store, amounts, first=0, last=32):
     sub = lax.broadcasted_iota(jnp.int32, (8, 128), 0)
     hits = [jnp.bitwise_and(sub, amount) for amount in amounts]
     keep_x = [hit == 0 for hit in hits]
@@ -306,12 +318,12 @@
                     vs[n] = jnp.where(keep_y[k], y, pltpu.roll(x, 8 - (1 << k), 0))
         return vs
 
-    block_loop(src, dst, load, store, work)
-
-
-def table_swaps(T, base, load, store):
+    block_loop(src, dst, load, store, work, first, last)
+
+
+def table_swaps(T, base, load, store, first=0, last=32):
     src, dst = table_strides(T, base)
-    sublane_swaps(src, dst, load, store, [T[base + 20 + k] for k in range(3)])
+    sublane_swaps(src, dst, load, store, [T[base + 20 + k] for k in range(3)], first, last)
 
 
 def transposes(T, base, load, store, first, last):
@@ -398,21 +410,27 @@
     return y + jnp.dot(xh, gh, preferred_element_type=jnp.float32)
 
 
-def split_kernel(perm, rho, out, T, buf):
-    step = pl.program_id(0)
-
-    @pl.when(step == 0)
-    def _():
-        make_plan_0(perm, T)
-
+def split_kernel(perm, rho, out, T, x, buf, buf2, sems):
+    fetches = []
     for c in range(8):
-        lanes = slice(c * 128, c * 128 + 128)
-        x = jnp.concatenate([rho[0, :, lanes], rho[1, :, lanes]], axis=0)
-        buf[pl.ds(pl.multiple_of(step * 1024 + c * 128, 128), 128), :] = x.T
-
-    @pl.when(step == 7)
-    def _():
-        table_swaps(T, S0, buf, out)
+        part = pl.ds(c * 1024, 1024)
+        fetches.append(pltpu.make_async_copy(rho.at[:, :, part], x.at[:, :, part], sems.at[0, c]))
+        fetches[-1].start()
+    make_plan_0(perm, T)
+    for c, fetch in enumerate(fetches):
+        fetch.wait()
+        for k in range(8):
+            lanes = slice(c * 1024 + k * 128, c * 1024 + k * 128 + 128)
+            block = jnp.concatenate([x[0, :, lanes], x[1, :, lanes]], axis=0)
+            buf[c * 1024 + k * 128 : c * 1024 + k * 128 + 128, :] = block.T
+    sends = []
+    for c in range(4):
+        table_swaps(T, S0, buf, buf2, 8 * c, 8 * c + 8)
+        rows = pl.ds(c * 2048, 2048)
+        sends.append(pltpu.make_async_copy(buf2.at[rows], out.at[rows], sems.at[1, c]))
+        sends[-1].start()
+    for send in sends:
+        send.wait()
 
 
 def prepare_kernel(first_table, sup, T, matrices):
@@ -588,10 +606,9 @@
 def per_device(rho, perm, superop):
     blocks, table = pl.pallas_call(
         split_kernel,
-        grid=(8,),
-        in_specs=[SMEM, pl.BlockSpec((2, 64, 1024), lambda i: (0, 0, i))],
-        out_specs=[pl.BlockSpec((8192, 128), lambda i: (0, 0)), SMEM],
-        scratch_shapes=[BUFFER],
+        in_specs=[SMEM, HBM],
+        out_specs=[HBM, SMEM],
+        scratch_shapes=[pltpu.VMEM((2, 64, 8192), jnp.float32), BUFFER, BUFFER, pltpu.SemaphoreType.DMA((2, 8))],
         out_shape=[
             jax.ShapeDtypeStruct((8192, 128), jnp.float32),
             jax.ShapeDtypeStruct((SIZE,), jnp.int32),

time: 187 us -> 182 us (0.973); the launches traced: 189 us -> 181 us
  Pallas kernels: 77.2 us -> 69.7 us
    pallas_call x1, Pallas kernels: 22.2 us -> 17.6 us  [per_device(): pl.pallas_call(first_kernel, in_specs=[SMEM, HBM, HBM], out_specs=VMEM, o...]
    pallas_call x1, Pallas kernels: 9.85 us -> 6.99 us  [per_device(): pl.pallas_call(split_kernel, in_specs=[SMEM, HBM], out_specs=[HBM, SMEM],...]
  transfers between devices with their start and end apart: 3 -> 3, of which waited for: 2 -> 2; matrix products, arithmetic and copies ran while one was open for 0% -> 0% of each run, Pallas kernels for 24% -> 25%
where the time goes in v5:
time: 182 us; the launch traced here: 181 us
  waiting for transfers between devices  83.3 us (46%)
  Pallas kernels  69.7 us (38%)
  starting transfers between devices  23.2 us (13%)
  between operations  2.5 us (1%)
  local copies, waits for them, and re-layouts  1.84 us (1%)
    all_to_all x3, waiting for transfers between devices, exchange(): return lax.all_to_all(blocks, AX, split_axis=0, concat_axis=0, tiled=True)  83.3 us
    all_to_all x3, starting transfers between devices, exchange(): return lax.all_to_all(blocks, AX, split_axis=0, concat_axis=0, tiled=True)  23.2 us
    pallas_call x1, Pallas kernels, per_device(): pl.pallas_call(second_kernel, in_specs=[SMEM, HBM, HBM], out_specs=HBM, o...  21 us
    pallas_call x1, Pallas kernels, per_device(): pl.pallas_call(first_kernel, in_specs=[SMEM, HBM, HBM], out_specs=VMEM, o...  17.6 us
    pallas_call x1, Pallas kernels, per_device(): pl.pallas_call(trace_kernel, grid=(16,), in_specs=[SMEM, SMEM, SMEM, pl.B...  15.1 us
    pallas_call x1, Pallas kernels, per_device(): pl.pallas_call(prepare_kernel, in_specs=[SMEM, VMEM], out_specs=[SMEM, VM...  8.96 us
    pallas_call x1, Pallas kernels, per_device(): pl.pallas_call(split_kernel, in_specs=[SMEM, HBM], out_specs=[HBM, SMEM],...  6.99 us
  transfers between devices with their start and end apart: 3, of which 2 were waited for; matrix products, arithmetic and copies ran while one was open for 0% of the time, Pallas kernels for 25%

profile of v5, /device:TPU:1, one launch (start us, length us, event | category | flops | bytes accessed | tf_op | source)
XLA Modules:
  0.0 181.3 jit_solution(15971638519646770991)
XLA Ops:
  0.6 7.0 %split.1 = (f32[8192,128]{1,0:T(8,128)}, s32[432]{0:T(512)}) custom-call(s32[2,13]{1,0:T(2,128)} %perm.1, f32[2,64,8192]{2,1,0:T(8,128)} %rho.1), custom_call_target="tpu_custom_call" | custom-call | tf_op jit(solution)/shard_map/split/pallas_call | solution.py:607
  7.6 12.0 %all-to-all-start = ((f32[128,64,128]{2,1,0:T(8,128)}), f32[128,64,128]{2,1,0:T(8,128)}, u32[]{:S(2)}, u32[]{:S(2)}) async-start(f32[128,64,128]{2,1,0:T(8,128)} %bitcast.15), calls=%async_computation | async-start | bytes 8388608 | tf_op jit(solution)/shard_map/all_to_all | solution.py:603
  19.6 9.0 %prepare.1 = (s32[432]{0:T(512)}, bf16[8,512,512]{2,1,0:T(8,128)(2,1)}) custom-call(s32[432]{0:T(512)} %get-tuple-element.8.first_table, f32[2,2,16,16]{3,2,1,0:T(8,128)} %sup.1), custom_call_target="tpu_custom_call" | custom-call | tf_op jit(solution)/shard_map/prepare/pallas_call | solution.py:619
  28.6 45.0 %all-to-all-done = f32[128,64,128]{2,1,0:T(8,128)} async-done(((f32[128,64,128]{2,1,0:T(8,128)}), f32[128,64,128]{2,1,0:T(8,128)}, u32[]{:S(2)}, u32[]{:S(2)}) %all-to-all-start) | async-done | bytes 4194336 | tf_op jit(solution)/shard_map/all_to_all | solution.py:603
  73.6 17.6 %first.1.x = f32[8192,128]{1,0:T(8,128)} custom-call(s32[432]{0:T(512)} %get-tuple-element.9.T, bf16[8,512,512]{2,1,0:T(8,128)(2,1)} %get-tuple-element.10.matrices_hbm, f32[8192,128]{1,0:T(8,128)} %bitcast.1.x), custom_call_target="tpu_custom_call" | custom-call | tf_op jit(solution)/shard_map/first/pallas_call | solution.py:631
  91.2 0.0 copy-start
  91.2 5.9 %all-to-all-start.1 = ((f32[128,64,128]{2,1,0:T(8,128)}), f32[128,64,128]{2,1,0:T(8,128)}, u32[]{:S(2)}, u32[]{:S(2)}) async-start(f32[128,64,128]{2,1,0:T(8,128)} %bitcast.13), calls=%async_computation.1 | async-start | bytes 8388608 | tf_op jit(solution)/shard_map/all_to_all | solution.py:603
  97.1 0.0 copy-done
  97.1 0.6 slice_bitcast_fusion.sup
  97.7 15.1 %trace.1 = f32[1,1]{1,0:T(1,128)} custom-call(s32[432]{0:T(512)} %get-tuple-element.9.T, s32[1]{0:T(128)} %bitcast.3.pos, f32[2,16,16]{2,1,0:T(8,128)} %slice_bitcast_fusion.sup, f32[8192,128]{1,0:T(8,128)} %first.1.x), custom_call_target="tpu_custom_call" | custom-call | tf_op jit(solution)/shard_map/trace/pallas_call | solution.py:641
  112.8 38.2 %all-to-all-done.1 = f32[128,64,128]{2,1,0:T(8,128)} async-done(((f32[128,64,128]{2,1,0:T(8,128)}), f32[128,64,128]{2,1,0:T(8,128)}, u32[]{:S(2)}, u32[]{:S(2)}) %all-to-all-start.1) | async-done | bytes 4194336 | tf_op jit(solution)/shard_map/all_to_all | solution.py:603
  151.1 1.2 broadcast_in_dim.3
  152.3 5.4 %all-to-all-start.2 = ((f32[128,1,128]{2,1,0:T(1,128)}), f32[128,1,128]{2,1,0:T(1,128)S(1)}, u32[]{:S(2)}, u32[]{:S(2)}) async-start(f32[128,1,128]{2,1,0:T(1,128)} %broadcast_in_dim.3), calls=%async_computation.2 | async-start | bytes 131072 | tf_op jit(solution)/shard_map/all_to_all | solution.py:603
  157.7 21.0 %second.1 = f32[16,512,128]{2,1,0:T(8,128)} custom-call(s32[432]{0:T(512)} %get-tuple-element.9.T, bf16[8,512,512]{2,1,0:T(8,128)(2,1)} %get-tuple-element.10.matrices_hbm, f32[8192,128]{1,0:T(8,128)} %bitcast.5.x), custom_call_target="tpu_custom_call" | custom-call | tf_op jit(solution)/shard_map/second/pallas_call | solution.py:652
  178.8 0.0 all-to-all-done.2
  178.8 0.7 slice_reduce_fusion
Async XLA Ops:
  7.6 66.0 %all-to-all-start = ((f32[128,64,128]{2,1,0:T(8,128)}), f32[128,64,128]{2,1,0:T(8,128)}, u32[]{:S(2)}, u32[]{:S(2)}) async-start(f32[128,64,128]{2,1,0:T(8,128)} %bitcast.15), calls=%async_computation | async-start | bytes 8388608 | tf_op jit(solution)/shard_map/all_to_all | solution.py:603
  91.2 5.9 %copy-start = (f32[2,2,16,16]{3,2,1,0:T(8,128)S(1)}, f32[2,2,16,16]{3,2,1,0:T(8,128)}, u32[]{:S(2)}) copy-start(f32[2,2,16,16]{3,2,1,0:T(8,128)} %sup.1) | copy-start | bytes 12292
  91.2 59.9 %all-to-all-start.1 = ((f32[128,64,128]{2,1,0:T(8,128)}), f32[128,64,128]{2,1,0:T(8,128)}, u32[]{:S(2)}, u32[]{:S(2)}) async-start(f32[128,64,128]{2,1,0:T(8,128)} %bitcast.13), calls=%async_computation.1 | async-start | bytes 8388608 | tf_op jit(solution)/shard_map/all_to_all | solution.py:603
  152.3 26.5 %all-to-all-start.2 = ((f32[128,1,128]{2,1,0:T(1,128)}), f32[128,1,128]{2,1,0:T(1,128)S(1)}, u32[]{:S(2)}, u32[]{:S(2)}) async-start(f32[128,1,128]{2,1,0:T(1,128)} %broadcast_in_dim.3), calls=%async_computation.2 | async-start | bytes 131072 | tf_op jit(solution)/shard_map/all_to_all | solution.py:603

commit v6 on v5

--- a/solution.py
+++ b/solution.py
@@ -529,7 +529,7 @@
         send.wait()
 
 
-def trace_kernel(T, pos, sup, x, out):
+def trace_kernel(T, pos, sup, x, out, acc):
     step = pl.program_id(0)
     lane = lax.broadcasted_iota(jnp.int32, (8, 128), 1)
     sub = lax.broadcasted_iota(jnp.int32, (8, 128), 0)
@@ -585,9 +585,13 @@
 
     @pl.when(step == 0)
     def _():
-        out[0, 0] = jnp.float32(0.0)
-
-    out[0, 0] = out[0, 0] + jnp.sum(total)
+        acc[0] = jnp.float32(0.0)
+
+    acc[0] = acc[0] + jnp.sum(total)
+
+    @pl.when(step == 15)
+    def _():
+        out[...] = jnp.full((128, 1, 128), acc[0], jnp.float32)
 
 
 SMEM = pl.BlockSpec(memory_space=pltpu.SMEM)
@@ -642,13 +646,14 @@
         trace_kernel,
         grid=(16,),
         in_specs=[SMEM, SMEM, SMEM, pl.BlockSpec((512, 128), lambda i: (i, 0))],
-        out_specs=SMEM,
-        out_shape=jax.ShapeDtypeStruct((1, 1), jnp.float32),
+        out_specs=pl.BlockSpec((128, 1, 128), lambda i: (0, 0, 0)),
+        out_shape=jax.ShapeDtypeStruct((128, 1, 128), jnp.float32),
+        scratch_shapes=[pltpu.SMEM((1,), jnp.float32)],
         name="trace",
     )(table, device, superop[1], blocks)
     blocks = exchange(blocks.reshape(128, 64, 128))
     blocks, trace = lax.optimization_barrier((blocks, trace))
-    parts = exchange(jnp.broadcast_to(trace[0, 0], (128, 1, 128)))
+    parts = exchange(trace)
     tiles = pl.pallas_call(
         second_kernel,
         in_specs=[SMEM, HBM, HBM],

time: 182 us -> 181 us (level)
  no operation moved by 1% of the time
where the time goes in v6:
time: 181 us; the launch traced here: 180 us
  waiting for transfers between devices  83.2 us (46%)
  Pallas kernels  69.8 us (39%)
  starting transfers between devices  23.2 us (13%)
  between operations  2.49 us (1%)
    all_to_all x3, waiting for transfers between devices, exchange(): return lax.all_to_all(blocks, AX, split_axis=0, concat_axis=0, tiled=True)  83.2 us
    all_to_all x3, starting transfers between devices, exchange(): return lax.all_to_all(blocks, AX, split_axis=0, concat_axis=0, tiled=True)  23.2 us
    pallas_call x1, Pallas kernels, per_device(): pl.pallas_call(second_kernel, in_specs=[SMEM, HBM, HBM], out_specs=HBM, o...  21 us
    pallas_call x1, Pallas kernels, per_device(): pl.pallas_call(first_kernel, in_specs=[SMEM, HBM, HBM], out_specs=VMEM, o...  17.6 us
    pallas_call x1, Pallas kernels, per_device(): pl.pallas_call(trace_kernel, grid=(16,), in_specs=[SMEM, SMEM, SMEM, pl.B...  15.2 us
    pallas_call x1, Pallas kernels, per_device(): pl.pallas_call(prepare_kernel, in_specs=[SMEM, VMEM], out_specs=[SMEM, VM...  8.96 us
    pallas_call x1, Pallas kernels, per_device(): pl.pallas_call(split_kernel, in_specs=[SMEM, HBM], out_specs=[HBM, SMEM],...  6.99 us
  transfers between devices with their start and end apart: 3, of which 2 were waited for; matrix products, arithmetic and copies ran while one was open for 0% of the time, Pallas kernels for 25%

profile of v6, /device:TPU:1, one launch (start us, length us, event | category | flops | bytes accessed | tf_op | source)
XLA Modules:
  0.0 180.1 jit_solution(17833572064182676850)
XLA Ops:
  0.6 7.0 %split.1 = (f32[8192,128]{1,0:T(8,128)}, s32[432]{0:T(512)}) custom-call(s32[2,13]{1,0:T(2,128)} %perm.1, f32[2,64,8192]{2,1,0:T(8,128)} %rho.1), custom_call_target="tpu_custom_call" | custom-call | tf_op jit(solution)/shard_map/split/pallas_call | solution.py:611
  7.6 12.0 %all-to-all-start = ((f32[128,64,128]{2,1,0:T(8,128)}), f32[128,64,128]{2,1,0:T(8,128)}, u32[]{:S(2)}, u32[]{:S(2)}) async-start(f32[128,64,128]{2,1,0:T(8,128)} %bitcast.14), calls=%async_computation | async-start | bytes 8388608 | tf_op jit(solution)/shard_map/all_to_all | solution.py:607
  19.6 9.0 %prepare.1 = (s32[432]{0:T(512)}, bf16[8,512,512]{2,1,0:T(8,128)(2,1)}) custom-call(s32[432]{0:T(512)} %get-tuple-element.8.first_table, f32[2,2,16,16]{3,2,1,0:T(8,128)} %sup.1), custom_call_target="tpu_custom_call" | custom-call | tf_op jit(solution)/shard_map/prepare/pallas_call | solution.py:623
  28.6 45.0 %all-to-all-done = f32[128,64,128]{2,1,0:T(8,128)} async-done(((f32[128,64,128]{2,1,0:T(8,128)}), f32[128,64,128]{2,1,0:T(8,128)}, u32[]{:S(2)}, u32[]{:S(2)}) %all-to-all-start) | async-done | bytes 4194336 | tf_op jit(solution)/shard_map/all_to_all | solution.py:607
  73.6 17.6 %first.1.x = f32[8192,128]{1,0:T(8,128)} custom-call(s32[432]{0:T(512)} %get-tuple-element.9.T, bf16[8,512,512]{2,1,0:T(8,128)(2,1)} %get-tuple-element.10.matrices_hbm, f32[8192,128]{1,0:T(8,128)} %bitcast.1.x), custom_call_target="tpu_custom_call" | custom-call | tf_op jit(solution)/shard_map/first/pallas_call | solution.py:635
  91.2 0.0 copy-start
  91.2 5.9 %all-to-all-start.1 = ((f32[128,64,128]{2,1,0:T(8,128)}), f32[128,64,128]{2,1,0:T(8,128)}, u32[]{:S(2)}, u32[]{:S(2)}) async-start(f32[128,64,128]{2,1,0:T(8,128)} %bitcast.12), calls=%async_computation.1 | async-start | bytes 8388608 | tf_op jit(solution)/shard_map/all_to_all | solution.py:607
  97.1 0.0 copy-done
  97.1 0.6 slice_bitcast_fusion.sup
  97.7 15.2 %trace.1 = f32[128,1,128]{2,1,0:T(1,128)} custom-call(s32[432]{0:T(512)} %get-tuple-element.9.T, s32[1]{0:T(128)} %bitcast.3.pos, f32[2,16,16]{2,1,0:T(8,128)} %slice_bitcast_fusion.sup, f32[8192,128]{1,0:T(8,128)} %first.1.x), custom_call_target="tpu_custom_call" | custom-call | tf_op jit(solution)/shard_map/trace/pallas_call | solution.py:645
  112.9 38.2 %all-to-all-done.1 = f32[128,64,128]{2,1,0:T(8,128)} async-done(((f32[128,64,128]{2,1,0:T(8,128)}), f32[128,64,128]{2,1,0:T(8,128)}, u32[]{:S(2)}, u32[]{:S(2)}) %all-to-all-start.1) | async-done | bytes 4194336 | tf_op jit(solution)/shard_map/all_to_all | solution.py:607
  151.1 5.4 %all-to-all-start.2 = ((f32[128,1,128]{2,1,0:T(1,128)}), f32[128,1,128]{2,1,0:T(1,128)S(1)}, u32[]{:S(2)}, u32[]{:S(2)}) async-start(f32[128,1,128]{2,1,0:T(1,128)} %trace.1), calls=%async_computation.2 | async-start | bytes 131072 | tf_op jit(solution)/shard_map/all_to_all | solution.py:607
  156.5 21.0 %second.1 = f32[16,512,128]{2,1,0:T(8,128)} custom-call(s32[432]{0:T(512)} %get-tuple-element.9.T, bf16[8,512,512]{2,1,0:T(8,128)(2,1)} %get-tuple-element.10.matrices_hbm, f32[8192,128]{1,0:T(8,128)} %bitcast.5.x), custom_call_target="tpu_custom_call" | custom-call | tf_op jit(solution)/shard_map/second/pallas_call | solution.py:657
  177.5 0.0 all-to-all-done.2
  177.5 0.7 slice_reduce_fusion
Async XLA Ops:
  7.6 66.0 %all-to-all-start = ((f32[128,64,128]{2,1,0:T(8,128)}), f32[128,64,128]{2,1,0:T(8,128)}, u32[]{:S(2)}, u32[]{:S(2)}) async-start(f32[128,64,128]{2,1,0:T(8,128)} %bitcast.14), calls=%async_computation | async-start | bytes 8388608 | tf_op jit(solution)/shard_map/all_to_all | solution.py:607
  91.2 5.9 %copy-start = (f32[2,2,16,16]{3,2,1,0:T(8,128)S(1)}, f32[2,2,16,16]{3,2,1,0:T(8,128)}, u32[]{:S(2)}) copy-start(f32[2,2,16,16]{3,2,1,0:T(8,128)} %sup.1) | copy-start | bytes 12292
  91.2 59.9 %all-to-all-start.1 = ((f32[128,64,128]{2,1,0:T(8,128)}), f32[128,64,128]{2,1,0:T(8,128)}, u32[]{:S(2)}, u32[]{:S(2)}) async-start(f32[128,64,128]{2,1,0:T(8,128)} %bitcast.12), calls=%async_computation.1 | async-start | bytes 8388608 | tf_op jit(solution)/shard_map/all_to_all | solution.py:607
  151.1 26.5 %all-to-all-start.2 = ((f32[128,1,128]{2,1,0:T(1,128)}), f32[128,1,128]{2,1,0:T(1,128)S(1)}, u32[]{:S(2)}, u32[]{:S(2)}) async-start(f32[128,1,128]{2,1,0:T(1,128)} %trace.1), calls=%async_computation.2 | async-start | bytes 131072 | tf_op jit(solution)/shard_map/all_to_all | solution.py:607
